TPU v7x, 512 devices: a 4x2x32 block of a 4x8x32 slice. The times are simulated.
512 devices in a mesh: grp: 2 (over y), lon: 32 (over z), view: 8 (over x, core).
Axes of the slice: x: 4, y: 2, z: 32, core: 2. Of those that a mesh axis runs over, the one named last changes fastest.
The devices are a block of a 4x8x32 slice.
Arguments:
- light_field: bfloat16 [128, 8, 1024, 128], P(('grp', 'view'), None, 'lon'), parts along dimension 0, may hold values from -6 to 6
- spatial_weights: bfloat16 [3, 3, 3, 128, 128], replicated, may hold values from -0.1875 to 0.1875
- spatial_offsets: float32 [3, 128], replicated, may hold values from -3 to 3
- angular_weight: bfloat16 [3, 3, 128, 128], replicated, may hold values from -0.1875 to 0.1875
- angular_offset: float32 [128], replicated, may hold values from -3 to 3
Outputs:
- refined: bfloat16 [128, 8, 1024, 128], P(('grp', 'view'), None, 'lon'), parts along dimension 0
There are 2 independent parts, one for each index of `grp`. A program takes and returns all parts, laid end to end along the dimension named above; an argument that names none is the same for every part. Nothing has to cross between parts.
All inputs are finite; a program needn't handle non-finite values.
Results may differ from a plain program's by a relative error of at most 0.0047.
Values may be sent and summed in bfloat16 or wider, within the bound.
No kernel may reach another device: no remote copies, remote signals or barrier semaphores. Data moves between devices by JAX's collectives and lax.ppermute only.
A program may use at most 64 MiB of HBM per device.

v0:
```python
import jax
import jax.numpy as jnp
from jax import lax
from jax.sharding import PartitionSpec as P

ANG = 8


def with_halo(cells, sides, width, closed):
    for axis, dim in sides:
        count = lax.axis_size(axis)
        ends = count if closed else count - 1
        head = lax.slice_in_dim(cells, 0, width, axis=dim)
        tail = lax.slice_in_dim(cells, cells.shape[dim] - width, cells.shape[dim], axis=dim)
        cells = jnp.concatenate(
            [
                lax.ppermute(tail, axis, [(i, (i + 1) % count) for i in range(ends)]),
                cells,
                lax.ppermute(head, axis, [((i + 1) % count, i) for i in range(ends)]),
            ],
            axis=dim,
        )
    return cells


def spatial_layer(widened, weight, offset):
    count, rows, wide_cols, chans = widened.shape
    cols = wide_cols - 2
    padded = jnp.pad(widened, ((0, 0), (1, 1), (0, 0), (0, 0)))
    total = jnp.zeros((count * rows * cols, chans), jnp.float32)
    for row_tap in range(3):
        stacked = jnp.concatenate(
            [padded[:, row_tap : row_tap + rows, col_tap : col_tap + cols] for col_tap in range(3)],
            axis=-1,
        )
        total = total + jnp.dot(
            stacked.reshape(-1, 3 * chans),
            weight[row_tap].reshape(3 * chans, chans),
            preferred_element_type=jnp.float32,
        )
    total = total.reshape(count, rows, cols, chans) + offset
    return jax.nn.gelu(total, approximate=True).astype(jnp.bfloat16)


def angular_layer(padded_rows, weight, offset):
    chans = padded_rows.shape[-1]
    grid_rows = padded_rows.shape[0] - 2
    views_grid = padded_rows.reshape(grid_rows + 2, ANG, -1, chans)
    padded = jnp.pad(views_grid, ((0, 0), (1, 1), (0, 0), (0, 0)))
    total = jnp.zeros((grid_rows * ANG * views_grid.shape[2], chans), jnp.float32)
    for row_tap in range(3):
        stacked = jnp.concatenate(
            [
                padded[row_tap : row_tap + grid_rows, col_tap : col_tap + ANG]
                for col_tap in range(3)
            ],
            axis=-1,
        )
        total = total + jnp.dot(
            stacked.reshape(-1, 3 * chans),
            weight[row_tap].reshape(3 * chans, chans),
            preferred_element_type=jnp.float32,
        )
    return (total + offset).astype(jnp.bfloat16)


def local(light_field, spatial_weights, spatial_offsets, angular_weight, angular_offset):
    layer_count = spatial_weights.shape[0]
    hidden = light_field
    for layer_index in range(layer_count):
        widened = with_halo(hidden, (("lon", 2),), 1, True)
        hidden = spatial_layer(widened, spatial_weights[layer_index], spatial_offsets[layer_index])
    chans = hidden.shape[-1]
    grid_rows = hidden.shape[0] // ANG
    shaped = hidden.reshape(grid_rows, ANG, hidden.shape[1], hidden.shape[2], chans)
    bordered = with_halo(shaped, (("view", 0),), 1, False)
    angular = angular_layer(bordered, angular_weight, angular_offset).reshape(hidden.shape)
    angular = lax.optimization_barrier(angular)
    return (light_field.astype(jnp.float32) + angular.astype(jnp.float32)).astype(jnp.bfloat16)


def solution(mesh):
    return jax.shard_map(
        local,
        mesh=mesh,
        in_specs=(P(("grp", "view"), None, "lon", None), P(), P(), P(), P()),
        out_specs=P(("grp", "view"), None, "lon", None),
        check_vma=False,
    )
```

profile of v0, /device:TPU:33, one launch (start us, length us, event | category | flops | bytes accessed | tf_op | source)
XLA Modules:
  0.0 100.4 jit_solution(10788288135427151308)
XLA Ops:
  0.0 1.1 %fusion.91 = (bf16[8,8,1,128]{3,2,1,0:T(2,128)(2,1)S(1)}, bf16[8,8,1,128]{3,2,1,0:T(2,128)(2,1)S(1)}) fusion(bf16[8,8,32,128]{3,2,1,0:T(8,128)(2,1)} %param.5), kind=kLoop, calls=%fused_computation.126 | loop fusion | bytes 65536 | tf_op jit(solution)/shard_map/slice | solution.py:14
  1.1 5.3 %collective-permute-start = (bf16[8,8,1,128]{3,2,1,0:T(2,128)(2,1)S(1)}, bf16[8,8,1,128]{3,2,1,0:T(2,128)(2,1)S(1)}, u32[]{:S(2)}, u32[]{:S(2)}) collective-permute-start(bf16[8,8,1,128]{3,2,1,0:T(2,128)(2,1)S(1)} %get-tuple-element.42), channel_id=1, source_target_pairs={{0,8},{8,16},{16,24},{24,32},{32,40},{40,48},{48,56},{56,64},{64,7... | collective-permute-start | bytes 49160 | tf_op jit(solution)/shard_map/ppermute | solution.py:17
  6.4 42.6 %collective-permute-start.1 = (bf16[8,8,1,128]{3,2,1,0:T(2,128)(2,1)S(1)}, bf16[8,8,1,128]{3,2,1,0:T(2,128)(2,1)S(1)}, u32[]{:S(2)}, u32[]{:S(2)}) collective-permute-start(bf16[8,8,1,128]{3,2,1,0:T(2,128)(2,1)S(1)} %get-tuple-element.43), channel_id=1, source_target_pairs={{8,0},{16,8},{24,16},{32,24},{40,32},{48,40},{56,48},{64,56},{72,6... | collective-permute-start | bytes 49160 | tf_op jit(solution)/shard_map/ppermute | solution.py:19
  48.9 1.3 %fusion.85 = (bf16[1,1,3,128,128]{4,3,2,1,0:T(8,128)(2,1)S(1)}, bf16[1,1,3,128,128]{4,3,2,1,0:T(8,128)(2,1)S(1)}, bf16[1,1,3,128,128]{4,3,2,1,0:T(8,128)(2,1)S(1...) fusion(bf16[3,3,3,128,128]{4,3,2,1,0:T(8,128)(2,1)} %param.6), kind=kLoop, calls=%fused_computation.120 | loop fusion | bytes 1769472 | tf_op jit(solution)/shard_map/slice | solution.py:38
  50.7 0.7 fusion.88
  52.5 0.7 fusion.13
  53.2 0.6 convolution_add_fusion.7
  53.8 0.6 convolution_add_fusion.6
  54.8 2.0 %collective-permute-start.2 = (bf16[8,8,1,128]{3,2,1,0:T(2,128)(2,1)S(1)}, bf16[8,8,1,128]{3,2,1,0:T(2,128)(2,1)S(1)}, u32[]{:S(2)}, u32[]{:S(2)}) collective-permute-start(bf16[8,8,1,128]{3,2,1,0:T(2,128)(2,1)S(1)} %get-tuple-element.40), channel_id=1, source_target_pairs={{0,8},{8,16},{16,24},{24,32},{32,40},{40,48},{48,56},{56,64},{64,7... | collective-permute-start | bytes 49160 | tf_op jit(solution)/shard_map/ppermute | solution.py:17
  56.8 4.6 %collective-permute-start.3 = (bf16[8,8,1,128]{3,2,1,0:T(2,128)(2,1)S(1)}, bf16[8,8,1,128]{3,2,1,0:T(2,128)(2,1)S(1)}, u32[]{:S(2)}, u32[]{:S(2)}) collective-permute-start(bf16[8,8,1,128]{3,2,1,0:T(2,128)(2,1)S(1)} %get-tuple-element.41), channel_id=1, source_target_pairs={{8,0},{16,8},{24,16},{32,24},{40,32},{48,40},{56,48},{64,56},{72,6... | collective-permute-start | bytes 49160 | tf_op jit(solution)/shard_map/ppermute | solution.py:19
  61.4 1.0 collective-permute-done.3
  62.7 0.7 fusion.87
  64.5 0.7 fusion.11
  65.2 0.6 convolution_add_fusion.5
  65.8 0.6 convolution_add_fusion.4
  66.8 2.0 %collective-permute-start.4 = (bf16[8,8,1,128]{3,2,1,0:T(2,128)(2,1)S(1)}, bf16[8,8,1,128]{3,2,1,0:T(2,128)(2,1)S(1)}, u32[]{:S(2)}, u32[]{:S(2)}) collective-permute-start(bf16[8,8,1,128]{3,2,1,0:T(2,128)(2,1)S(1)} %get-tuple-element.38), channel_id=1, source_target_pairs={{0,8},{8,16},{16,24},{24,32},{32,40},{40,48},{48,56},{56,64},{64,7... | collective-permute-start | bytes 49160 | tf_op jit(solution)/shard_map/ppermute | solution.py:17
  68.8 5.1 %collective-permute-start.5 = (bf16[8,8,1,128]{3,2,1,0:T(2,128)(2,1)S(1)}, bf16[8,8,1,128]{3,2,1,0:T(2,128)(2,1)S(1)}, u32[]{:S(2)}, u32[]{:S(2)}) collective-permute-start(bf16[8,8,1,128]{3,2,1,0:T(2,128)(2,1)S(1)} %get-tuple-element.39), channel_id=1, source_target_pairs={{8,0},{16,8},{24,16},{32,24},{40,32},{48,40},{56,48},{64,56},{72,6... | collective-permute-start | bytes 49160 | tf_op jit(solution)/shard_map/ppermute | solution.py:19
  73.9 0.8 collective-permute-done.5
  75.0 0.7 fusion.86
  76.0 0.6 fusion.95
  76.8 0.7 fusion.9
  77.5 0.6 convolution_add_fusion.3
  78.1 0.8 fusion.70
  79.3 6.8 %collective-permute-start.6 = (bf16[1,8,8,32,128]{4,3,2,1,0:T(8,128)(2,1)S(1)}, bf16[1,8,8,32,128]{4,3,2,1,0:T(8,128)(2,1)S(1)}, u32[]{:S(2)}, u32[]{:S(2)}) collective-permute-start(bf16[1,8,8,32,128]{4,3,2,1,0:T(8,128)(2,1)S(1)} %fusion.54), channel_id=1, source_target_pairs={{0,1},{1,2},{2,3},{3,4},{4,5},{5,6},{6,7},{8,9},{9,10},{10,11},{11... | collective-permute-start | bytes 1572872 | tf_op jit(solution)/shard_map/ppermute | solution.py:17
  86.1 2.0 %collective-permute-start.7 = (bf16[1,8,8,32,128]{4,3,2,1,0:T(8,128)(2,1)S(1)}, bf16[1,8,8,32,128]{4,3,2,1,0:T(8,128)(2,1)S(1)}, u32[]{:S(2)}, u32[]{:S(2)}) collective-permute-start(bf16[1,8,8,32,128]{4,3,2,1,0:T(8,128)(2,1)S(1)} %fusion.54), channel_id=1, source_target_pairs={{1,0},{2,1},{3,2},{4,3},{5,4},{6,5},{7,6},{9,8},{10,9},{11,10},{12... | collective-permute-start | bytes 1572872 | tf_op jit(solution)/shard_map/ppermute | solution.py:19
  88.5 3.7 %collective-permute-done.6 = bf16[1,8,8,32,128]{4,3,2,1,0:T(8,128)(2,1)S(1)} collective-permute-done((bf16[1,8,8,32,128]{4,3,2,1,0:T(8,128)(2,1)S(1)}, bf16[1,8,8,32,128]{4,3,2,1,0:T(8,128)(2,1)S(1)}, u32[]{:S(2)}, u32[]{:S(2)}) %collective-permute-start.6) | collective-permute-done | bytes 524320 | tf_op jit(solution)/shard_map/ppermute | solution.py:17
  92.3 4.4 %collective-permute-done.7 = bf16[1,8,8,32,128]{4,3,2,1,0:T(8,128)(2,1)S(1)} collective-permute-done((bf16[1,8,8,32,128]{4,3,2,1,0:T(8,128)(2,1)S(1)}, bf16[1,8,8,32,128]{4,3,2,1,0:T(8,128)(2,1)S(1)}, u32[]{:S(2)}, u32[]{:S(2)}) %collective-permute-start.7) | collective-permute-done | bytes 524320 | tf_op jit(solution)/shard_map/ppermute | solution.py:19
  96.9 0.7 fusion.84
  97.6 0.6 fusion.20
  98.2 0.6 convolution_add_fusion.1
  98.8 0.6 fusion.2
  99.4 0.9 add_convert_fusion
  (31 shorter events, 5.6 us)
Async XLA Ops:
  0.0 50.3 %copy-start = (bf16[8,8,32,128]{3,2,1,0:T(8,128)(2,1)S(1)}, bf16[8,8,32,128]{3,2,1,0:T(8,128)(2,1)}, u32[]{:S(2)}) copy-start(bf16[8,8,32,128]{3,2,1,0:T(8,128)(2,1)} %param.5) | copy-start | bytes 1572868
  0.0 50.3 %copy-start.2 = (f32[3,128]{1,0:T(4,128)S(1)}, f32[3,128]{1,0:T(4,128)}, u32[]{:S(2)}) copy-start(f32[3,128]{1,0:T(4,128)} %param.7) | copy-start | bytes 4612
  1.1 49.2 %collective-permute-start = (bf16[8,8,1,128]{3,2,1,0:T(2,128)(2,1)S(1)}, bf16[8,8,1,128]{3,2,1,0:T(2,128)(2,1)S(1)}, u32[]{:S(2)}, u32[]{:S(2)}) collective-permute-start(bf16[8,8,1,128]{3,2,1,0:T(2,128)(2,1)S(1)} %get-tuple-element.42), channel_id=1, source_target_pairs={{0,8},{8,16},{16,24},{24,32},{32,40},{40,48},{48,56},{56,64},{64,7... | collective-permute-start | bytes 49160 | tf_op jit(solution)/shard_map/ppermute | solution.py:17
  6.4 44.0 %collective-permute-start.1 = (bf16[8,8,1,128]{3,2,1,0:T(2,128)(2,1)S(1)}, bf16[8,8,1,128]{3,2,1,0:T(2,128)(2,1)S(1)}, u32[]{:S(2)}, u32[]{:S(2)}) collective-permute-start(bf16[8,8,1,128]{3,2,1,0:T(2,128)(2,1)S(1)} %get-tuple-element.43), channel_id=1, source_target_pairs={{8,0},{16,8},{24,16},{32,24},{40,32},{48,40},{56,48},{64,56},{72,6... | collective-permute-start | bytes 49160 | tf_op jit(solution)/shard_map/ppermute | solution.py:19
  54.8 6.6 %collective-permute-start.2 = (bf16[8,8,1,128]{3,2,1,0:T(2,128)(2,1)S(1)}, bf16[8,8,1,128]{3,2,1,0:T(2,128)(2,1)S(1)}, u32[]{:S(2)}, u32[]{:S(2)}) collective-permute-start(bf16[8,8,1,128]{3,2,1,0:T(2,128)(2,1)S(1)} %get-tuple-element.40), channel_id=1, source_target_pairs={{0,8},{8,16},{16,24},{24,32},{32,40},{40,48},{48,56},{56,64},{64,7... | collective-permute-start | bytes 49160 | tf_op jit(solution)/shard_map/ppermute | solution.py:17
  56.8 5.6 %collective-permute-start.3 = (bf16[8,8,1,128]{3,2,1,0:T(2,128)(2,1)S(1)}, bf16[8,8,1,128]{3,2,1,0:T(2,128)(2,1)S(1)}, u32[]{:S(2)}, u32[]{:S(2)}) collective-permute-start(bf16[8,8,1,128]{3,2,1,0:T(2,128)(2,1)S(1)} %get-tuple-element.41), channel_id=1, source_target_pairs={{8,0},{16,8},{24,16},{32,24},{40,32},{48,40},{56,48},{64,56},{72,6... | collective-permute-start | bytes 49160 | tf_op jit(solution)/shard_map/ppermute | solution.py:19
  66.8 7.0 %collective-permute-start.4 = (bf16[8,8,1,128]{3,2,1,0:T(2,128)(2,1)S(1)}, bf16[8,8,1,128]{3,2,1,0:T(2,128)(2,1)S(1)}, u32[]{:S(2)}, u32[]{:S(2)}) collective-permute-start(bf16[8,8,1,128]{3,2,1,0:T(2,128)(2,1)S(1)} %get-tuple-element.38), channel_id=1, source_target_pairs={{0,8},{8,16},{16,24},{24,32},{32,40},{40,48},{48,56},{56,64},{64,7... | collective-permute-start | bytes 49160 | tf_op jit(solution)/shard_map/ppermute | solution.py:17
  68.8 5.9 %collective-permute-start.5 = (bf16[8,8,1,128]{3,2,1,0:T(2,128)(2,1)S(1)}, bf16[8,8,1,128]{3,2,1,0:T(2,128)(2,1)S(1)}, u32[]{:S(2)}, u32[]{:S(2)}) collective-permute-start(bf16[8,8,1,128]{3,2,1,0:T(2,128)(2,1)S(1)} %get-tuple-element.39), channel_id=1, source_target_pairs={{8,0},{16,8},{24,16},{32,24},{40,32},{48,40},{56,48},{64,56},{72,6... | collective-permute-start | bytes 49160 | tf_op jit(solution)/shard_map/ppermute | solution.py:19
  78.9 9.2 %copy-start.1 = (bf16[3,3,128,128]{3,2,1,0:T(8,128)(2,1)S(1)}, bf16[3,3,128,128]{3,2,1,0:T(8,128)(2,1)}, u32[]{:S(2)}) copy-start(bf16[3,3,128,128]{3,2,1,0:T(8,128)(2,1)} %param.8) | copy-start | bytes 884740
  79.3 12.9 %collective-permute-start.6 = (bf16[1,8,8,32,128]{4,3,2,1,0:T(8,128)(2,1)S(1)}, bf16[1,8,8,32,128]{4,3,2,1,0:T(8,128)(2,1)S(1)}, u32[]{:S(2)}, u32[]{:S(2)}) collective-permute-start(bf16[1,8,8,32,128]{4,3,2,1,0:T(8,128)(2,1)S(1)} %fusion.54), channel_id=1, source_target_pairs={{0,1},{1,2},{2,3},{3,4},{4,5},{5,6},{6,7},{8,9},{9,10},{10,11},{11... | collective-permute-start | bytes 1572872 | tf_op jit(solution)/shard_map/ppermute | solution.py:17
  86.1 10.5 %collective-permute-start.7 = (bf16[1,8,8,32,128]{4,3,2,1,0:T(8,128)(2,1)S(1)}, bf16[1,8,8,32,128]{4,3,2,1,0:T(8,128)(2,1)S(1)}, u32[]{:S(2)}, u32[]{:S(2)}) collective-permute-start(bf16[1,8,8,32,128]{4,3,2,1,0:T(8,128)(2,1)S(1)} %fusion.54), channel_id=1, source_target_pairs={{1,0},{2,1},{3,2},{4,3},{5,4},{6,5},{7,6},{9,8},{10,9},{11,10},{12... | collective-permute-start | bytes 1572872 | tf_op jit(solution)/shard_map/ppermute | solution.py:19
  98.2 0.7 copy-start.3
where the time goes:
time: 101 us; the launch traced here: 100 us
  starting transfers between devices  70.2 us (70%)
  waiting for transfers between devices  9.95 us (10%)
  other arithmetic  7.28 us (7%)
  matrix products  7.14 us (7%)
  local copies, waits for them, and re-layouts  5.38 us (5%)
    ppermute x4, starting transfers between devices, with_halo(): lax.ppermute(head, axis, [((i + 1) % count, i) for i in range(ends)])  54.2 us
    ppermute x4, starting transfers between devices, with_halo(): lax.ppermute(tail, axis, [(i, (i + 1) % count) for i in range(ends)])  16 us
    ppermute x4, waiting for transfers between devices, with_halo(): lax.ppermute(head, axis, [((i + 1) % count, i) for i in range(ends)])  6.23 us
    dot_general x9, matrix products, spatial_layer(): jnp.dot(stacked.reshape(-1, 3 * chans), weight[row_tap].reshape(3 * chans...  5.41 us
    ppermute x4, waiting for transfers between devices, with_halo(): lax.ppermute(tail, axis, [(i, (i + 1) % count) for i in range(ends)])  3.72 us
    concatenate x8, other arithmetic, spatial_layer(): jnp.concatenate([padded[:, row_tap:row_tap + rows, col_tap:col_tap + cols...  3.52 us
    slice x3, local copies, waits for them, and re-layouts, spatial_layer(): padded[:, row_tap:row_tap + rows, col_tap:col_tap + cols]  2.06 us
  transfers between devices with their start and end apart: 8, of which 4 were waited for; matrix products, arithmetic and copies ran while one was open for 2% of the time, Pallas kernels for 0%

commit v1 on v0

v1 whole, which is shorter than its diff:
```python
import functools

import jax
import jax.numpy as jnp
from jax import lax
from jax.experimental import pallas as pl
from jax.experimental.pallas import tpu as pltpu
from jax.sharding import PartitionSpec as P

EDGE = 4
HALO = 2 * EDGE


def gelu(t):
    half = 0.5 * t
    return half + half * jnp.tanh(t * (0.7978845608 + (0.7978845608 * 0.044715) * (t * t)))


def put_shifted(dst, row, cells, views, cols):
    for shift, moved in ((0, pltpu.roll(cells, 1, 1)), (1, cells), (2, pltpu.roll(cells, cols + HALO - 1, 1))):
        chans = cells.shape[-1]
        dst[shift, row, : views * cols] = moved[:, :cols].reshape(views * cols, chans).astype(dst.dtype)
        dst[shift, row, views * cols :] = moved[:, cols:].reshape(views * HALO, chans).astype(dst.dtype)


def hidden_kernel(side_ref, field_ref, near_ref, far_ref, weight_ref, offset_ref, out_ref, even, odd):
    views, rows, cols, chans = field_ref.shape
    layers = weight_ref.shape[0]
    own = views * cols
    for buf in (even, odd):
        for shift in range(3):
            for row in (0, rows + 1):
                buf[shift, row] = jnp.zeros(buf.shape[2:], buf.dtype)
    first = side_ref[0] == 0
    for row in range(rows):
        near = near_ref[:, row].astype(jnp.float32)
        far = far_ref[:, row].astype(jnp.float32)
        right = jnp.where(first, near, far)
        left = jnp.where(first, far, near)
        cells = jnp.concatenate([field_ref[:, row].astype(jnp.float32), right, left], axis=1)
        put_shifted(even, row + 1, cells, views, cols)
    blank = jnp.zeros((chans, chans), weight_ref.dtype)
    bufs = (even, odd)
    for layer in range(layers):
        src, dst = bufs[layer % 2], bufs[(layer + 1) % 2]
        last = layer == layers - 1
        span = own if last else own + views * HALO
        weight = jnp.concatenate(
            [
                jnp.concatenate(
                    [weight_ref[layer, k, b] if k < 3 else blank, weight_ref[layer, k - 1, b] if k > 0 else blank],
                    axis=1,
                )
                for k in range(4)
                for b in range(3)
            ],
            axis=0,
        )
        offset = offset_ref[layer]
        for pair in range(rows // 2):
            stacked = jnp.concatenate(
                [src[b, 2 * pair + k, :span] for k in range(4) for b in range(3)], axis=1
            )
            total = jnp.dot(stacked, weight, preferred_element_type=jnp.float32)
            for r in range(2):
                value = gelu(total[:, r * chans : (r + 1) * chans] + offset)
                row = 2 * pair + r
                if last:
                    out_ref[row] = value.astype(out_ref.dtype)
                else:
                    cells = jnp.concatenate(
                        [value[:own].reshape(views, cols, chans), value[own:].reshape(views, HALO, chans)], axis=1
                    )
                    put_shifted(dst, row + 1, cells, views, cols)


def angular_kernel(side_ref, hidden_ref, far_ref, near_ref, weight_ref, offset_ref, field_ref, out_hbm, out, sems):
    views, rows, cols, chans = field_ref.shape
    even = side_ref[0] == 0
    far_tap = jnp.where(even, 0, 2)
    near_tap = 2 - far_tap
    sources = ((hidden_ref, 1), (near_ref, near_tap), (far_ref, far_tap))
    offset = offset_ref[...]
    blank = jnp.zeros((chans, chans), weight_ref.dtype)
    copies = []
    for pair in range(views // 2):
        stacked, weight = [], []
        for ref, tap in sources:
            for k in range(4):
                view = 2 * pair + k - 1
                if 0 <= view < views:
                    stacked.append(ref[:, view * cols : (view + 1) * cols].reshape(rows * cols, chans))
                    weight.append(
                        jnp.concatenate(
                            [weight_ref[tap, k] if k < 3 else blank, weight_ref[tap, k - 1] if k > 0 else blank],
                            axis=1,
                        )
                    )
        total = jnp.dot(
            jnp.concatenate(stacked, axis=1), jnp.concatenate(weight, axis=0), preferred_element_type=jnp.float32
        )
        for r in range(2):
            view = 2 * pair + r
            angular = (total[:, r * chans : (r + 1) * chans] + offset).astype(jnp.bfloat16)
            field = field_ref[view].reshape(rows * cols, chans).astype(jnp.float32)
            out[view] = (field + angular.astype(jnp.float32)).astype(out.dtype).reshape(rows, cols, chans)
        part = pl.ds(2 * pair, 2)
        copies.append(pltpu.make_async_copy(out.at[part], out_hbm.at[part], sems.at[pair]))
        copies[-1].start()
    for copy in copies:
        copy.wait()


VMEM = pl.BlockSpec(memory_space=pltpu.VMEM)
SMEM = pl.BlockSpec(memory_space=pltpu.SMEM)


def swap(cells, axis, start, count, closed):
    pairs = []
    for i in range(start, count, 2):
        j = i + 1
        if j < count or closed:
            pairs += [(i, j % count), (j % count, i)]
    return lax.ppermute(cells, axis, pairs)


def local(light_field, spatial_weights, spatial_offsets, angular_weight, angular_offset):
    views, rows, cols, chans = light_field.shape
    lon_count, view_count = lax.axis_size("lon"), lax.axis_size("view")
    lon_side = lax.rem(lax.axis_index("lon"), 2)
    view_side = lax.rem(lax.axis_index("view"), 2)
    head, tail = light_field[:, :, :EDGE], light_field[:, :, cols - EDGE :]
    far = swap(jnp.where(lon_side == 0, head, tail), "lon", 1, lon_count, True)
    near = swap(jnp.where(lon_side == 0, tail, head), "lon", 0, lon_count, True)
    span = views * (cols + HALO)
    hidden = pl.pallas_call(
        hidden_kernel,
        out_shape=jax.ShapeDtypeStruct((rows, views * cols, chans), jnp.bfloat16),
        in_specs=[SMEM, VMEM, VMEM, VMEM, VMEM, VMEM],
        out_specs=VMEM,
        scratch_shapes=[pltpu.VMEM((3, rows + 2, span, chans), jnp.bfloat16)] * 2,
        compiler_params=pltpu.CompilerParams(vmem_limit_bytes=24 * 2**20),
        name="hidden",
    )(lon_side[None], light_field, near, far, spatial_weights, spatial_offsets[:, None])
    far_rows = swap(hidden, "view", 1, view_count, False)
    near_rows = swap(hidden, "view", 0, view_count, False)
    return pl.pallas_call(
        angular_kernel,
        out_shape=jax.ShapeDtypeStruct(light_field.shape, jnp.bfloat16),
        in_specs=[SMEM, VMEM, VMEM, VMEM, VMEM, VMEM, VMEM],
        out_specs=pl.BlockSpec(memory_space=pl.ANY),
        scratch_shapes=[
            pltpu.VMEM(light_field.shape, jnp.bfloat16),
            pltpu.SemaphoreType.DMA((views // 2,)),
        ],
        compiler_params=pltpu.CompilerParams(vmem_limit_bytes=16 * 2**20),
        name="angular",
    )(view_side[None], hidden, far_rows, near_rows, angular_weight, angular_offset[None], light_field)


def solution(mesh):
    return jax.shard_map(
        local,
        mesh=mesh,
        in_specs=(P(("grp", "view"), None, "lon", None), P(), P(), P(), P()),
        out_specs=P(("grp", "view"), None, "lon", None),
        check_vma=False,
    )
```

time: 101 us -> 75.4 us (0.75)
  starting transfers between devices: 70.2 us -> 55 us
  matrix products: 7.14 us -> 0 us
  other arithmetic: 7.28 us -> 1.05 us
  Pallas kernels: 0 us -> 5.67 us
  local copies, waits for them, and re-layouts: 5.38 us -> 2.88 us
    ppermute x8 -> x4, starting transfers between devices: 70.2 us -> 55 us  [swap(): return lax.ppermute(cells, axis, pairs)]
    dot_general x12 -> x0, matrix products: 7.14 us -> none  [the longest x9 5.41 us: spatial_layer(): jnp.dot(stacked.reshape(-1, 3 * chans), weight[row_tap].reshape(3 * chans...]
    pallas_call x0 -> x2, Pallas kernels: none -> 5.67 us  [the longest x1 4 us: local(): pl.pallas_call(hidden_kernel, out_shape=jax.ShapeDtypeStruct((rows, views...]
    slice x9 -> x0, local copies, waits for them, and re-layouts: 5.31 us -> none  [the longest x3 2.06 us: spatial_layer(): padded[:, row_tap:row_tap + rows, col_tap:col_tap + cols]]
    concatenate x12 -> x0, other arithmetic: 4.81 us -> none  [the longest x8 3.52 us: spatial_layer(): jnp.concatenate([padded[:, row_tap:row_tap + rows, col_tap:col_tap + cols...]
    unnamed x8 -> x12, local copies, waits for them, and re-layouts: 0.07 us -> 2.87 us
    convert_element_type x5 -> x0, other arithmetic: 2.47 us -> none  [the longest x4 1.54 us: spatial_layer(): return jax.nn.gelu(total, approximate=True).astype(jnp.bfloat16)]
    select_n x0 -> x1, other arithmetic: none -> 1.05 us  [local(): far = swap(jnp.where(lon_side == 0, head, tail), 'lon', 1, lon_count, True)]
  transfers between devices with their start and end apart: 8 -> 4, of which waited for: 4 -> 2; matrix products, arithmetic and copies ran while one was open for 2% -> 0% of each run, Pallas kernels for 0% -> 0%
where the time goes in v1:
time: 75.4 us; the launch traced here: 75 us
  starting transfers between devices  55 us (73%)
  waiting for transfers between devices  10.4 us (14%)
  Pallas kernels  5.67 us (8%)
  local copies, waits for them, and re-layouts  2.88 us (4%)
  other arithmetic  1.05 us (1%)
    ppermute x4, starting transfers between devices, swap(): return lax.ppermute(cells, axis, pairs)  55 us
    ppermute x4, waiting for transfers between devices, swap(): return lax.ppermute(cells, axis, pairs)  10.4 us
    pallas_call x1, Pallas kernels, local(): pl.pallas_call(hidden_kernel, out_shape=jax.ShapeDtypeStruct((rows, views...  4 us
    unnamed x12, local copies, waits for them, and re-layouts  2.87 us
    pallas_call x1, Pallas kernels, local(): pl.pallas_call(angular_kernel, out_shape=jax.ShapeDtypeStruct(light_field...  1.66 us
  transfers between devices with their start and end apart: 4, of which 2 were waited for; matrix products, arithmetic and copies ran while one was open for 0% of the time, Pallas kernels for 0%

profile of v1, /device:TPU:33, one launch (start us, length us, event | category | flops | bytes accessed | tf_op | source)
XLA Modules:
  0.0 75.0 jit_solution(6646759021727793403)
XLA Ops:
  0.0 1.0 %broadcast_select_fusion = (bf16[8,8,4,128]{3,2,1,0:T(4,128)(2,1)S(1)}, bf16[8,8,4,128]{3,2,1,0:T(4,128)(2,1)S(1)}) fusion(pred[]{:T(512)S(6)} %eq.4, bf16[8,8,32,128]{3,2,1,0:T(8,128)(2,1)} %field_ref.3), kind=kLoop, calls=%fused_computation | loop fusion | flops 65536 | bytes 262145 | tf_op jit(solution)/shard_map/jit(_where)/select_n | solution.py:133
  1.1 0.0 copy-start.5
  1.1 45.9 %collective-permute-start.1 = (bf16[8,8,4,128]{3,2,1,0:T(4,128)(2,1)S(1)}, bf16[8,8,4,128]{3,2,1,0:T(4,128)(2,1)S(1)}, u32[]{:S(2)}, u32[]{:S(2)}) collective-permute-start(bf16[8,8,4,128]{3,2,1,0:T(4,128)(2,1)S(1)} %get-tuple-element.5), channel_id=1, source_target_pairs={{8,16},{16,8},{24,32},{32,24},{40,48},{48,40},{56,64},{64,56},{72,... | collective-permute-start | bytes 196616 | tf_op jit(solution)/shard_map/ppermute | solution.py:124
  46.9 2.0 %collective-permute-start = (bf16[8,8,4,128]{3,2,1,0:T(4,128)(2,1)S(1)}, bf16[8,8,4,128]{3,2,1,0:T(4,128)(2,1)S(1)}, u32[]{:S(2)}, u32[]{:S(2)}) collective-permute-start(bf16[8,8,4,128]{3,2,1,0:T(4,128)(2,1)S(1)} %get-tuple-element.6), channel_id=1, source_target_pairs={{0,8},{8,0},{16,24},{24,16},{32,40},{40,32},{48,56},{56,48},{64,72... | collective-permute-start | bytes 196616 | tf_op jit(solution)/shard_map/ppermute | solution.py:124
  48.9 0.0 copy-done.5
  48.9 0.0 collective-permute-done.1.far_ref
  48.9 3.0 %collective-permute-done.near_ref = bf16[8,8,4,128]{3,2,1,0:T(4,128)(2,1)S(1)} collective-permute-done((bf16[8,8,4,128]{3,2,1,0:T(4,128)(2,1)S(1)}, bf16[8,8,4,128]{3,2,1,0:T(4,128)(2,1)S(1)}, u32[]{:S(2)}, u32[]{:S(2)}) %collective-permute-start) | collective-permute-done | bytes 65568 | tf_op jit(solution)/shard_map/ppermute | solution.py:124
  52.0 0.0 copy-start
  52.0 1.0 %copy-done = bf16[8,8,32,128]{3,2,1,0:T(8,128)(2,1)S(1)} copy-done((bf16[8,8,32,128]{3,2,1,0:T(8,128)(2,1)S(1)}, bf16[8,8,32,128]{3,2,1,0:T(8,128)(2,1)}, u32[]{:S(2)}) %copy-start) | copy-done | bytes 524312
  53.0 0.0 copy-start.2
  53.0 1.2 %copy-done.2 = bf16[3,3,3,128,128]{4,3,2,1,0:T(8,128)(2,1)S(1)} copy-done((bf16[3,3,3,128,128]{4,3,2,1,0:T(8,128)(2,1)S(1)}, bf16[3,3,3,128,128]{4,3,2,1,0:T(8,128)(2,1)}, u32[]{:S(2)}) %copy-start.2) | copy-done | bytes 884760
  54.2 0.0 copy-start.1
  54.2 0.0 copy-start.3
  54.2 4.0 %hidden.1.hidden_ref = bf16[8,256,128]{2,1,0:T(8,128)(2,1)S(1)} custom-call(s32[1]{0:T(128)} %bitcast.1.side_ref, bf16[8,8,32,128]{3,2,1,0:T(8,128)(2,1)S(1)} %copy-done, bf16[8,8,4,128]{3,2,1,0:T(4,128)(2,1)S(1)} %collective-permute-done.near_ref, bf16[8,8,4,128]{3,2,1,0:T(4,128)(2,1)S(1)} %collective-permute-done.1.far_ref, ...), custom_call_target="tpu_custom_call" | custom-call | tf_op jit(solution)/shard_map/hidden/pallas_call | solution.py:136
  58.2 4.0 %collective-permute-start.3 = (bf16[8,256,128]{2,1,0:T(8,128)(2,1)S(1)}, bf16[8,256,128]{2,1,0:T(8,128)(2,1)S(1)}, u32[]{:S(2)}, u32[]{:S(2)}) collective-permute-start(bf16[8,256,128]{2,1,0:T(8,128)(2,1)S(1)} %hidden.1.hidden_ref), channel_id=1, source_target_pairs={{0,1},{1,0},{2,3},{3,2},{4,5},{5,4},{6,7},{7,6},{8,9},{9,8},{10,11... | collective-permute-start | bytes 1572872 | tf_op jit(solution)/shard_map/ppermute | solution.py:124
  62.2 3.2 %collective-permute-start.2 = (bf16[8,256,128]{2,1,0:T(8,128)(2,1)S(1)}, bf16[8,256,128]{2,1,0:T(8,128)(2,1)S(1)}, u32[]{:S(2)}, u32[]{:S(2)}) collective-permute-start(bf16[8,256,128]{2,1,0:T(8,128)(2,1)S(1)} %hidden.1.hidden_ref), channel_id=1, source_target_pairs={{1,2},{2,1},{3,4},{4,3},{5,6},{6,5},{9,10},{10,9},{11,12},{12,11},... | collective-permute-start | bytes 1572872 | tf_op jit(solution)/shard_map/ppermute | solution.py:124
  65.4 0.0 collective-permute-done.3.near_ref
  65.4 7.3 %collective-permute-done.2.far_ref = bf16[8,256,128]{2,1,0:T(8,128)(2,1)S(1)} collective-permute-done((bf16[8,256,128]{2,1,0:T(8,128)(2,1)S(1)}, bf16[8,256,128]{2,1,0:T(8,128)(2,1)S(1)}, u32[]{:S(2)}, u32[]{:S(2)}) %collective-permute-start.2) | collective-permute-done | bytes 524320 | tf_op jit(solution)/shard_map/ppermute | solution.py:124
  72.7 0.0 copy-start.4
  72.7 0.0 copy-done.1
  72.7 0.0 copy-done.3
  72.7 0.6 copy-done.4
  73.4 1.7 %angular.1 = bf16[8,8,32,128]{3,2,1,0:T(8,128)(2,1)} custom-call(s32[1]{0:T(128)} %bitcast.side_ref, bf16[8,256,128]{2,1,0:T(8,128)(2,1)S(1)} %hidden.1.hidden_ref, bf16[8,256,128]{2,1,0:T(8,128)(2,1)S(1)} %collective-permute-done.2.far_ref, bf16[8,256,128]{2,1,0:T(8,128)(2,1)S(1)} %collective-permute-done.3.near_ref, ...), custom_call_target="tpu_custom_call" | custom-call | tf_op jit(solution)/shard_map/angular/pallas_call | solution.py:147
  (1 shorter events, 0.0 us)
Async XLA Ops:
  1.1 47.9 %copy-start.5 = (f32[3,128]{1,0:T(4,128)S(1)}, f32[3,128]{1,0:T(4,128)}, u32[]{:S(2)}) copy-start(f32[3,128]{1,0:T(4,128)} %param.7) | copy-start | bytes 4612
  1.1 47.9 %collective-permute-start.1 = (bf16[8,8,4,128]{3,2,1,0:T(4,128)(2,1)S(1)}, bf16[8,8,4,128]{3,2,1,0:T(4,128)(2,1)S(1)}, u32[]{:S(2)}, u32[]{:S(2)}) collective-permute-start(bf16[8,8,4,128]{3,2,1,0:T(4,128)(2,1)S(1)} %get-tuple-element.5), channel_id=1, source_target_pairs={{8,16},{16,8},{24,32},{32,24},{40,48},{48,40},{56,64},{64,56},{72,... | collective-permute-start | bytes 196616 | tf_op jit(solution)/shard_map/ppermute | solution.py:124
  46.9 5.0 %collective-permute-start = (bf16[8,8,4,128]{3,2,1,0:T(4,128)(2,1)S(1)}, bf16[8,8,4,128]{3,2,1,0:T(4,128)(2,1)S(1)}, u32[]{:S(2)}, u32[]{:S(2)}) collective-permute-start(bf16[8,8,4,128]{3,2,1,0:T(4,128)(2,1)S(1)} %get-tuple-element.6), channel_id=1, source_target_pairs={{0,8},{8,0},{16,24},{24,16},{32,40},{40,32},{48,56},{56,48},{64,72... | collective-permute-start | bytes 196616 | tf_op jit(solution)/shard_map/ppermute | solution.py:124
  52.0 1.0 %copy-start = (bf16[8,8,32,128]{3,2,1,0:T(8,128)(2,1)S(1)}, bf16[8,8,32,128]{3,2,1,0:T(8,128)(2,1)}, u32[]{:S(2)}) copy-start(bf16[8,8,32,128]{3,2,1,0:T(8,128)(2,1)} %field_ref.3) | copy-start | bytes 1572868
  53.0 1.2 %copy-start.2 = (bf16[3,3,3,128,128]{4,3,2,1,0:T(8,128)(2,1)S(1)}, bf16[3,3,3,128,128]{4,3,2,1,0:T(8,128)(2,1)}, u32[]{:S(2)}) copy-start(bf16[3,3,3,128,128]{4,3,2,1,0:T(8,128)(2,1)} %weight_ref.2) | copy-start | bytes 2654212
  54.2 18.5 %copy-start.1 = (bf16[8,8,32,128]{3,2,1,0:T(8,128)(2,1)S(1)}, bf16[8,8,32,128]{3,2,1,0:T(8,128)(2,1)}, u32[]{:S(2)}) copy-start(bf16[8,8,32,128]{3,2,1,0:T(8,128)(2,1)} %field_ref.3) | copy-start | bytes 1572868
  54.2 18.5 %copy-start.3 = (bf16[3,3,128,128]{3,2,1,0:T(8,128)(2,1)S(1)}, bf16[3,3,128,128]{3,2,1,0:T(8,128)(2,1)}, u32[]{:S(2)}) copy-start(bf16[3,3,128,128]{3,2,1,0:T(8,128)(2,1)} %weight_ref.3) | copy-start | bytes 884740
  58.2 7.2 %collective-permute-start.3 = (bf16[8,256,128]{2,1,0:T(8,128)(2,1)S(1)}, bf16[8,256,128]{2,1,0:T(8,128)(2,1)S(1)}, u32[]{:S(2)}, u32[]{:S(2)}) collective-permute-start(bf16[8,256,128]{2,1,0:T(8,128)(2,1)S(1)} %hidden.1.hidden_ref), channel_id=1, source_target_pairs={{0,1},{1,0},{2,3},{3,2},{4,5},{5,4},{6,7},{7,6},{8,9},{9,8},{10,11... | collective-permute-start | bytes 1572872 | tf_op jit(solution)/shard_map/ppermute | solution.py:124
  62.2 10.5 %collective-permute-start.2 = (bf16[8,256,128]{2,1,0:T(8,128)(2,1)S(1)}, bf16[8,256,128]{2,1,0:T(8,128)(2,1)S(1)}, u32[]{:S(2)}, u32[]{:S(2)}) collective-permute-start(bf16[8,256,128]{2,1,0:T(8,128)(2,1)S(1)} %hidden.1.hidden_ref), channel_id=1, source_target_pairs={{1,2},{2,1},{3,4},{4,3},{5,6},{6,5},{9,10},{10,9},{11,12},{12,11},... | collective-permute-start | bytes 1572872 | tf_op jit(solution)/shard_map/ppermute | solution.py:124
  72.7 0.7 copy-start.4

commit v2 on v1

v2 whole, which is shorter than its diff:
```python
import jax
import jax.numpy as jnp
from jax import lax
from jax.experimental import pallas as pl
from jax.experimental.pallas import tpu as pltpu
from jax.sharding import PartitionSpec as P


EDGE = 4
TILE = 8
GROUPS = 4
VMEM = pl.BlockSpec(memory_space=pltpu.VMEM)
SMEM = pl.BlockSpec(memory_space=pltpu.SMEM)
HBM = pl.BlockSpec(memory_space=pl.ANY)


def gelu(t):
    half = 0.5 * t
    return half + half * jnp.tanh(t * (0.7978845608 + (0.7978845608 * 0.044715) * (t * t)))


def pair_weight(block, blank, count):
    return jnp.concatenate(
        [
            jnp.concatenate([block(k, b) if k < 3 else blank, block(k - 1, b) if k > 0 else blank], axis=1)
            for k in range(4)
            for b in range(count)
        ],
        axis=0,
    )


def spatial_weight(weight_ref, layer):
    blank = jnp.zeros(weight_ref.shape[-2:], weight_ref.dtype)
    return pair_weight(lambda k, b: weight_ref[layer, k, b], blank, 3)


def put_shifted(dst, row, cells):
    groups, width, chans = cells.shape
    for shift, moved in ((0, pltpu.roll(cells, 1, 1)), (1, cells), (2, pltpu.roll(cells, width - 1, 1))):
        dst[shift, row] = moved.reshape(groups * width, chans).astype(dst.dtype)


def clear_borders(buf):
    for shift in range(3):
        for row in (0, buf.shape[1] - 1):
            buf[shift, row] = jnp.zeros(buf.shape[2:], buf.dtype)


def edge_tile(cells):
    first, last = cells[:, :TILE], cells[:, cells.shape[1] - TILE :]
    place = lax.broadcasted_iota(jnp.int32, first.shape, 1)
    return pltpu.roll(jnp.where(place < EDGE, first, last), EDGE, 1)


def pack_kernel(side_ref, field_hbm, near_ref, far_ref, tiles, sems):
    cols = field_hbm.shape[2]
    copies = [
        pltpu.make_async_copy(field_hbm.at[:, :, pl.ds(start, TILE)], tiles.at[i], sems.at[i])
        for i, start in enumerate((0, cols - TILE))
    ]
    for copy in copies:
        copy.start()
    for copy in copies:
        copy.wait()
    first = side_ref[0] == 0
    for view in range(tiles.shape[1]):
        head = tiles[0, view].astype(jnp.float32)[:, :EDGE]
        tail = tiles[1, view].astype(jnp.float32)[:, TILE - EDGE :]
        near_ref[view] = jnp.where(first, tail, head).astype(near_ref.dtype)
        far_ref[view] = jnp.where(first, head, tail).astype(far_ref.dtype)


def inner_kernel(field_ref, weight_ref, offset_ref, out_ref, saved_ref, even, odd):
    views, rows, cols, chans = field_ref.shape
    layers = weight_ref.shape[0]
    bufs = (even, odd)
    for buf in bufs:
        clear_borders(buf)
    for row in range(rows):
        cells = field_ref[:, row].astype(jnp.float32)
        put_shifted(even, row + 1, cells)
        saved_ref[0, row] = edge_tile(cells).reshape(views * TILE, chans).astype(saved_ref.dtype)
    for layer in range(layers):
        src, dst = bufs[layer % 2], bufs[(layer + 1) % 2]
        weight = spatial_weight(weight_ref, layer)
        offset = offset_ref[layer]
        for pair in range(rows // 2):
            stacked = jnp.concatenate([src[b, 2 * pair + k] for k in range(4) for b in range(3)], axis=1)
            total = jnp.dot(stacked, weight, preferred_element_type=jnp.float32)
            for r in range(2):
                value = gelu(total[:, r * chans : (r + 1) * chans] + offset)
                row = 2 * pair + r
                if layer == layers - 1:
                    out_ref[row] = value.astype(out_ref.dtype)
                else:
                    cells = value.reshape(views, cols, chans)
                    put_shifted(dst, row + 1, cells)
                    saved_ref[layer + 1, row] = (
                        edge_tile(cells).reshape(views * TILE, chans).astype(saved_ref.dtype)
                    )


def outer_kernel(side_ref, near_ref, far_ref, saved_ref, inner_ref, weight_ref, offset_ref, out_ref, even, odd):
    all_views, rows, _, chans = near_ref.shape
    layers = weight_ref.shape[0]
    cols = inner_ref.shape[1] // all_views
    bufs = (even, odd)
    groups = even.shape[0]
    views = all_views // groups
    first = side_ref[0] == 0
    place = lax.broadcasted_iota(jnp.int32, (views, TILE, chans), 1)

    def kept(layer, row, group):
        part = saved_ref[layer, row, group * views * TILE : (group + 1) * views * TILE]
        return part.astype(jnp.float32).reshape(views, TILE, chans)

    for group in range(groups):
        for buf in bufs:
            clear_borders(buf.at[group])
        span = slice(group * views, (group + 1) * views)
        for row in range(rows):
            near = near_ref[span, row].astype(jnp.float32)
            far = far_ref[span, row].astype(jnp.float32)
            right = jnp.where(first, near, far)
            left = jnp.where(first, far, near)
            own = kept(0, row, group)
            cells = jnp.concatenate([left, own[:, EDGE:], own[:, :EDGE], right], axis=1)
            put_shifted(even.at[group], row + 1, cells)
    for layer in range(layers):
        weight = spatial_weight(weight_ref, layer)
        offset = offset_ref[layer]
        for group in range(groups):
            src, dst = bufs[layer % 2].at[group], bufs[(layer + 1) % 2].at[group]
            stacked = jnp.concatenate(
                [
                    jnp.concatenate([src[b, 2 * pair + k] for pair in range(rows // 2)], axis=0)
                    for k in range(4)
                    for b in range(3)
                ],
                axis=1,
            )
            total = jnp.dot(stacked, weight, preferred_element_type=jnp.float32)
            span = views * 2 * TILE
            for row in range(rows):
                part = total[(row // 2) * span : (row // 2 + 1) * span, (row % 2) * chans : (row % 2 + 1) * chans]
                value = gelu(part + offset).reshape(views, 2 * TILE, chans)
                lower, upper = value[:, :TILE], value[:, TILE:]
                if layer == layers - 1:
                    part = slice(group * views * cols, (group + 1) * views * cols)
                    cells = inner_ref[row, part].astype(jnp.float32).reshape(views, cols, chans)
                    fresh = layers
                    lower = jnp.where(place < fresh, pltpu.roll(lower, EDGE, 1), cells[:, :TILE])
                    upper = jnp.where(place >= TILE - fresh, pltpu.roll(upper, EDGE, 1), cells[:, cols - TILE :])
                    cells = jnp.concatenate([lower, cells[:, TILE : cols - TILE], upper], axis=1)
                    out_ref[row, part] = cells.reshape(views * cols, chans).astype(out_ref.dtype)
                else:
                    own = kept(layer + 1, row, group)
                    lower = jnp.where(place > EDGE + layer, own, lower)
                    upper = jnp.where(place < EDGE - 1 - layer, own, upper)
                    put_shifted(dst, row + 1, jnp.concatenate([lower, upper], axis=1))


def view_pair(sources, pair, views, cols, chans, blank):
    stacked, weight = [], []
    for ref, taps in sources:
        for k in range(4):
            view = 2 * pair + k - 1
            if 0 <= view < views:
                stacked.append(ref[:, view * cols : (view + 1) * cols].reshape(-1, chans))
                weight.append(
                    jnp.concatenate([taps(k) if k < 3 else blank, taps(k - 1) if k > 0 else blank], axis=1)
                )
    return jnp.dot(
        jnp.concatenate(stacked, axis=1), jnp.concatenate(weight, axis=0), preferred_element_type=jnp.float32
    )


def partial_kernel(side_ref, hidden_ref, near_ref, weight_ref, offset_ref, out_ref):
    pairs, _, wide = out_ref.shape
    chans = wide // 2
    views = 2 * pairs
    cols = hidden_ref.shape[1] // views
    near_tap = jnp.where(side_ref[0] == 0, 2, 0)
    blank = jnp.zeros((chans, chans), weight_ref.dtype)
    offset = jnp.concatenate([offset_ref[...]] * 2, axis=1)
    sources = ((hidden_ref, lambda k: weight_ref[1, k]), (near_ref, lambda k: weight_ref[near_tap, k]))
    for pair in range(pairs):
        out_ref[pair] = view_pair(sources, pair, views, cols, chans, blank) + offset


def final_kernel(side_ref, far_ref, partial_ref, weight_ref, field_ref, out_hbm, out, sems):
    views, rows, cols, chans = field_ref.shape
    far_tap = jnp.where(side_ref[0] == 0, 0, 2)
    blank = jnp.zeros((chans, chans), weight_ref.dtype)
    sources = ((far_ref, lambda k: weight_ref[far_tap, k]),)
    copies = []
    for pair in range(views // 2):
        total = view_pair(sources, pair, views, cols, chans, blank) + partial_ref[pair]
        for r in range(2):
            view = 2 * pair + r
            angular = total[:, r * chans : (r + 1) * chans].astype(jnp.bfloat16)
            field = field_ref[view].reshape(rows * cols, chans).astype(jnp.float32)
            out[view] = (field + angular.astype(jnp.float32)).astype(out.dtype).reshape(rows, cols, chans)
        part = pl.ds(2 * pair, 2)
        copies.append(pltpu.make_async_copy(out.at[part], out_hbm.at[part], sems.at[pair]))
        copies[-1].start()
    for copy in copies:
        copy.wait()


def swap(cells, axis, start, count, closed):
    pairs = []
    for i in range(start, count, 2):
        j = i + 1
        if j < count or closed:
            pairs += [(i, j % count), (j % count, i)]
    return lax.ppermute(cells, axis, pairs)


def params(mebibytes):
    return pltpu.CompilerParams(vmem_limit_bytes=mebibytes * 2**20)


def local(light_field, spatial_weights, spatial_offsets, angular_weight, angular_offset):
    views, rows, cols, chans = light_field.shape
    lon_count, view_count = lax.axis_size("lon"), lax.axis_size("view")
    lon_side = lax.rem(lax.axis_index("lon"), 2)[None]
    view_side = lax.rem(lax.axis_index("view"), 2)[None]
    offsets = spatial_offsets[:, None]
    layers = spatial_weights.shape[0]
    half = jnp.bfloat16

    edge = jax.ShapeDtypeStruct((views, rows, EDGE, chans), half)
    near, far = pl.pallas_call(
        pack_kernel,
        out_shape=(edge, edge),
        in_specs=[SMEM, HBM],
        out_specs=(VMEM, VMEM),
        scratch_shapes=[
            pltpu.VMEM((2, views, rows, TILE, chans), half),
            pltpu.SemaphoreType.DMA((2,)),
        ],
        compiler_params=params(4),
        name="pack",
    )(lon_side, pltpu.with_memory_space_constraint(light_field, pltpu.HBM))
    far = swap(far, "lon", 1, lon_count, True)
    near = swap(near, "lon", 0, lon_count, True)

    inner, saved = pl.pallas_call(
        inner_kernel,
        out_shape=(
            jax.ShapeDtypeStruct((rows, views * cols, chans), half),
            jax.ShapeDtypeStruct((layers, rows, views * TILE, chans), half),
        ),
        in_specs=[VMEM] * 3,
        out_specs=(VMEM, VMEM),
        scratch_shapes=[pltpu.VMEM((3, rows + 2, views * cols, chans), half)] * 2,
        compiler_params=params(20),
        name="inner",
    )(light_field, spatial_weights, offsets)
    hidden = pl.pallas_call(
        outer_kernel,
        out_shape=jax.ShapeDtypeStruct((rows, views * cols, chans), half),
        in_specs=[SMEM] + [VMEM] * 6,
        out_specs=VMEM,
        scratch_shapes=[pltpu.VMEM((GROUPS, 3, rows + 2, views // GROUPS * 2 * TILE, chans), half)] * 2,
        compiler_params=params(16),
        name="outer",
    )(lon_side, near, far, saved, inner, spatial_weights, offsets)

    far_rows = swap(hidden, "view", 1, view_count, False)
    near_rows = swap(hidden, "view", 0, view_count, False)
    partial = pl.pallas_call(
        partial_kernel,
        out_shape=jax.ShapeDtypeStruct((views // 2, rows * cols, 2 * chans), jnp.float32),
        in_specs=[SMEM] + [VMEM] * 4,
        out_specs=VMEM,
        compiler_params=params(8),
        name="partial",
    )(view_side, hidden, near_rows, angular_weight, angular_offset[None])
    return pl.pallas_call(
        final_kernel,
        out_shape=jax.ShapeDtypeStruct(light_field.shape, half),
        in_specs=[SMEM] + [VMEM] * 4,
        out_specs=HBM,
        scratch_shapes=[
            pltpu.VMEM(light_field.shape, half),
            pltpu.SemaphoreType.DMA((views // 2,)),
        ],
        compiler_params=params(8),
        name="final",
    )(view_side, far_rows, partial, angular_weight, light_field)


def solution(mesh):
    return jax.shard_map(
        local,
        mesh=mesh,
        in_specs=(P(("grp", "view"), None, "lon", None), P(), P(), P(), P()),
        out_specs=P(("grp", "view"), None, "lon", None),
        check_vma=False,
    )
```

time: 75.4 us -> 70.7 us (0.938)
  waiting for transfers between devices: 10.4 us -> 6.03 us
  Pallas kernels: 5.67 us -> 8.43 us
  local copies, waits for them, and re-layouts: 2.88 us -> 1.82 us
  other arithmetic: 1.05 us -> 0 us
  starting transfers between devices: 55 us -> 54 us
    ppermute x4, waiting for transfers between devices: 10.4 us -> 6.03 us  [swap(): return lax.ppermute(cells, axis, pairs)]
    pallas_call x2 -> x5, Pallas kernels: 5.67 us -> 8.43 us  [the longest x1 3.52 us: local(): pl.pallas_call(inner_kernel, out_shape=(jax.ShapeDtypeStruct((rows, views...]
    unnamed x12 -> x10, local copies, waits for them, and re-layouts: 2.87 us -> 1.82 us
    select_n x1 -> x0, other arithmetic: 1.05 us -> none  [local(): far = swap(jnp.where(lon_side == 0, head, tail), 'lon', 1, lon_count, True)]
    ppermute x4, starting transfers between devices: 55 us -> 54 us  [swap(): return lax.ppermute(cells, axis, pairs)]
  transfers between devices with their start and end apart: 4 -> 4, of which waited for: 2 -> 1; matrix products, arithmetic and copies ran while one was open for 0% -> 0% of each run, Pallas kernels for 0% -> 6%
where the time goes in v2:
time: 70.7 us; the launch traced here: 70.4 us
  starting transfers between devices  54 us (76%)
  Pallas kernels  8.43 us (12%)
  waiting for transfers between devices  6.03 us (9%)
  local copies, waits for them, and re-layouts  1.82 us (3%)
    ppermute x4, starting transfers between devices, swap(): return lax.ppermute(cells, axis, pairs)  54 us
    ppermute x4, waiting for transfers between devices, swap(): return lax.ppermute(cells, axis, pairs)  6.03 us
    pallas_call x1, Pallas kernels, local(): pl.pallas_call(inner_kernel, out_shape=(jax.ShapeDtypeStruct((rows, views...  3.52 us
    pallas_call x1, Pallas kernels, local(): pl.pallas_call(outer_kernel, out_shape=jax.ShapeDtypeStruct((rows, views...  1.92 us
    unnamed x10, local copies, waits for them, and re-layouts  1.82 us
  transfers between devices with their start and end apart: 4, of which 1 were waited for; matrix products, arithmetic and copies ran while one was open for 0% of the time, Pallas kernels for 6%

profile of v2, /device:TPU:33, one launch (start us, length us, event | category | flops | bytes accessed | tf_op | source)
XLA Modules:
  0.0 70.4 jit_solution(5120048632093688177)
XLA Ops:
  0.0 0.0 copy-start
  0.0 1.1 %pack.1 = (bf16[8,8,4,128]{3,2,1,0:T(4,128)(2,1)S(1)}, bf16[8,8,4,128]{3,2,1,0:T(4,128)(2,1)S(1)}) custom-call(s32[1]{0:T(128)} %bitcast.1.side_ref, bf16[8,8,32,128]{3,2,1,0:T(8,128)(2,1)} %field_ref.3), custom_call_target="tpu_custom_call" | custom-call | tf_op jit(solution)/shard_map/pack/pallas_call | solution.py:235
  1.1 0.0 copy-start.4
  1.2 5.3 %collective-permute-start = (bf16[8,8,4,128]{3,2,1,0:T(4,128)(2,1)S(1)}, bf16[8,8,4,128]{3,2,1,0:T(4,128)(2,1)S(1)}, u32[]{:S(2)}, u32[]{:S(2)}) collective-permute-start(bf16[8,8,4,128]{3,2,1,0:T(4,128)(2,1)S(1)} %get-tuple-element.9), channel_id=1, source_target_pairs={{0,8},{8,0},{16,24},{24,16},{32,40},{40,32},{48,56},{56,48},{64,72... | collective-permute-start | bytes 196616 | tf_op jit(solution)/shard_map/ppermute | solution.py:218
  6.4 42.6 %collective-permute-start.1 = (bf16[8,8,4,128]{3,2,1,0:T(4,128)(2,1)S(1)}, bf16[8,8,4,128]{3,2,1,0:T(4,128)(2,1)S(1)}, u32[]{:S(2)}, u32[]{:S(2)}) collective-permute-start(bf16[8,8,4,128]{3,2,1,0:T(4,128)(2,1)S(1)} %get-tuple-element.10), channel_id=1, source_target_pairs={{8,16},{16,8},{24,32},{32,24},{40,48},{48,40},{56,64},{64,56},{72,... | collective-permute-start | bytes 196616 | tf_op jit(solution)/shard_map/ppermute | solution.py:218
  49.0 0.0 copy-done.4
  49.0 0.0 copy-done
  49.0 0.0 copy-start.1
  49.0 1.2 %copy-done.1 = bf16[3,3,3,128,128]{4,3,2,1,0:T(8,128)(2,1)S(1)} copy-done((bf16[3,3,3,128,128]{4,3,2,1,0:T(8,128)(2,1)S(1)}, bf16[3,3,3,128,128]{4,3,2,1,0:T(8,128)(2,1)}, u32[]{:S(2)}) %copy-start.1) | copy-done | bytes 884760
  50.2 3.5 %inner.1 = (bf16[8,256,128]{2,1,0:T(8,128)(2,1)S(1)}, bf16[3,8,64,128]{3,2,1,0:T(8,128)(2,1)S(1)}) custom-call(bf16[8,8,32,128]{3,2,1,0:T(8,128)(2,1)S(1)} %copy-done, bf16[3,3,3,128,128]{4,3,2,1,0:T(8,128)(2,1)S(1)} %copy-done.1, f32[3,1,128]{2,1,0:T(1,128)S(1)} %broadcast_in_dim.14.offset_ref), custom_call_target="tpu_custom_call" | custom-call | tf_op jit(solution)/shard_map/inner/pallas_call | solution.py:250
  53.7 0.0 collective-permute-done.near_ref
  53.7 0.0 collective-permute-done.1.far_ref
  53.7 0.0 copy-start.2
  53.8 1.9 %outer.1.hidden_ref = bf16[8,256,128]{2,1,0:T(8,128)(2,1)S(1)} custom-call(s32[1]{0:T(128)} %bitcast.1.side_ref, bf16[8,8,4,128]{3,2,1,0:T(4,128)(2,1)S(1)} %collective-permute-done.near_ref, bf16[8,8,4,128]{3,2,1,0:T(4,128)(2,1)S(1)} %collective-permute-done.1.far_ref, bf16[3,8,64,128]{3,2,1,0:T(8,128)(2,1)S(1)} %get-tuple-element.11.saved_ref, ...), custom_call_target="tpu_custom_call" | custom-call | tf_op jit(solution)/shard_map/outer/pallas_call | solution.py:262
  55.7 3.0 %collective-permute-start.3 = (bf16[8,256,128]{2,1,0:T(8,128)(2,1)S(1)}, bf16[8,256,128]{2,1,0:T(8,128)(2,1)S(1)}, u32[]{:S(2)}, u32[]{:S(2)}) collective-permute-start(bf16[8,256,128]{2,1,0:T(8,128)(2,1)S(1)} %outer.1.hidden_ref), channel_id=1, source_target_pairs={{0,1},{1,0},{2,3},{3,2},{4,5},{5,4},{6,7},{7,6},{8,9},{9,8},{10,11... | collective-permute-start | bytes 1572872 | tf_op jit(solution)/shard_map/ppermute | solution.py:218
  58.7 3.2 %collective-permute-start.2 = (bf16[8,256,128]{2,1,0:T(8,128)(2,1)S(1)}, bf16[8,256,128]{2,1,0:T(8,128)(2,1)S(1)}, u32[]{:S(2)}, u32[]{:S(2)}) collective-permute-start(bf16[8,256,128]{2,1,0:T(8,128)(2,1)S(1)} %outer.1.hidden_ref), channel_id=1, source_target_pairs={{1,2},{2,1},{3,4},{4,3},{5,6},{6,5},{9,10},{10,9},{11,12},{12,11},... | collective-permute-start | bytes 1572872 | tf_op jit(solution)/shard_map/ppermute | solution.py:218
  61.9 0.0 collective-permute-done.3.near_ref
  61.9 0.0 copy-start.3
  61.9 0.0 copy-done.2
  61.9 0.6 copy-done.3
  62.5 0.6 partial.1.partial_ref
  63.2 6.0 %collective-permute-done.2.far_ref = bf16[8,256,128]{2,1,0:T(8,128)(2,1)S(1)} collective-permute-done((bf16[8,256,128]{2,1,0:T(8,128)(2,1)S(1)}, bf16[8,256,128]{2,1,0:T(8,128)(2,1)S(1)}, u32[]{:S(2)}, u32[]{:S(2)}) %collective-permute-start.2) | collective-permute-done | bytes 524320 | tf_op jit(solution)/shard_map/ppermute | solution.py:218
  69.2 1.2 %final.1 = bf16[8,8,32,128]{3,2,1,0:T(8,128)(2,1)} custom-call(s32[1]{0:T(128)} %bitcast.side_ref, bf16[8,256,128]{2,1,0:T(8,128)(2,1)S(1)} %collective-permute-done.2.far_ref, f32[4,256,256]{2,1,0:T(8,128)S(1)} %partial.1.partial_ref, bf16[3,3,128,128]{3,2,1,0:T(8,128)(2,1)S(1)} %copy-done.2, bf16[8,8,32,128]{3,2,1,0:T(8,128)(2,1)S(1)} %copy-done), custom_call_target="tpu_custom_call" | custom-call | tf_op jit(solution)/shard_map/final/pallas_call | solution.py:282
  (1 shorter events, 0.0 us)
Async XLA Ops:
  0.0 49.0 %copy-start = (bf16[8,8,32,128]{3,2,1,0:T(8,128)(2,1)S(1)}, bf16[8,8,32,128]{3,2,1,0:T(8,128)(2,1)}, u32[]{:S(2)}) copy-start(bf16[8,8,32,128]{3,2,1,0:T(8,128)(2,1)} %field_ref.3) | copy-start | bytes 1572868
  1.1 47.9 %copy-start.4 = (f32[3,128]{1,0:T(4,128)S(1)}, f32[3,128]{1,0:T(4,128)}, u32[]{:S(2)}) copy-start(f32[3,128]{1,0:T(4,128)} %param.7) | copy-start | bytes 4612
  1.2 52.6 %collective-permute-start = (bf16[8,8,4,128]{3,2,1,0:T(4,128)(2,1)S(1)}, bf16[8,8,4,128]{3,2,1,0:T(4,128)(2,1)S(1)}, u32[]{:S(2)}, u32[]{:S(2)}) collective-permute-start(bf16[8,8,4,128]{3,2,1,0:T(4,128)(2,1)S(1)} %get-tuple-element.9), channel_id=1, source_target_pairs={{0,8},{8,0},{16,24},{24,16},{32,40},{40,32},{48,56},{56,48},{64,72... | collective-permute-start | bytes 196616 | tf_op jit(solution)/shard_map/ppermute | solution.py:218
  6.4 47.3 %collective-permute-start.1 = (bf16[8,8,4,128]{3,2,1,0:T(4,128)(2,1)S(1)}, bf16[8,8,4,128]{3,2,1,0:T(4,128)(2,1)S(1)}, u32[]{:S(2)}, u32[]{:S(2)}) collective-permute-start(bf16[8,8,4,128]{3,2,1,0:T(4,128)(2,1)S(1)} %get-tuple-element.10), channel_id=1, source_target_pairs={{8,16},{16,8},{24,32},{32,24},{40,48},{48,40},{56,64},{64,56},{72,... | collective-permute-start | bytes 196616 | tf_op jit(solution)/shard_map/ppermute | solution.py:218
  49.0 1.2 %copy-start.1 = (bf16[3,3,3,128,128]{4,3,2,1,0:T(8,128)(2,1)S(1)}, bf16[3,3,3,128,128]{4,3,2,1,0:T(8,128)(2,1)}, u32[]{:S(2)}) copy-start(bf16[3,3,3,128,128]{4,3,2,1,0:T(8,128)(2,1)} %weight_ref.5) | copy-start | bytes 2654212
  53.7 8.1 %copy-start.2 = (bf16[3,3,128,128]{3,2,1,0:T(8,128)(2,1)S(1)}, bf16[3,3,128,128]{3,2,1,0:T(8,128)(2,1)}, u32[]{:S(2)}) copy-start(bf16[3,3,128,128]{3,2,1,0:T(8,128)(2,1)} %weight_ref.7) | copy-start | bytes 884740
  55.7 6.2 %collective-permute-start.3 = (bf16[8,256,128]{2,1,0:T(8,128)(2,1)S(1)}, bf16[8,256,128]{2,1,0:T(8,128)(2,1)S(1)}, u32[]{:S(2)}, u32[]{:S(2)}) collective-permute-start(bf16[8,256,128]{2,1,0:T(8,128)(2,1)S(1)} %outer.1.hidden_ref), channel_id=1, source_target_pairs={{0,1},{1,0},{2,3},{3,2},{4,5},{5,4},{6,7},{7,6},{8,9},{9,8},{10,11... | collective-permute-start | bytes 1572872 | tf_op jit(solution)/shard_map/ppermute | solution.py:218
  58.7 10.5 %collective-permute-start.2 = (bf16[8,256,128]{2,1,0:T(8,128)(2,1)S(1)}, bf16[8,256,128]{2,1,0:T(8,128)(2,1)S(1)}, u32[]{:S(2)}, u32[]{:S(2)}) collective-permute-start(bf16[8,256,128]{2,1,0:T(8,128)(2,1)S(1)} %outer.1.hidden_ref), channel_id=1, source_target_pairs={{1,2},{2,1},{3,4},{4,3},{5,6},{6,5},{9,10},{10,9},{11,12},{12,11},... | collective-permute-start | bytes 1572872 | tf_op jit(solution)/shard_map/ppermute | solution.py:218
  61.9 0.7 copy-start.3

commit v3 on v2

v3 whole, which is shorter than its diff:
```python
import jax
import jax.numpy as jnp
from jax import lax
from jax.experimental import pallas as pl
from jax.experimental.pallas import tpu as pltpu
from jax.sharding import PartitionSpec as P


EDGE = 4
TILE = 8
GROUPS = 4
VMEM = pl.BlockSpec(memory_space=pltpu.VMEM)
SMEM = pl.BlockSpec(memory_space=pltpu.SMEM)
HBM = pl.BlockSpec(memory_space=pl.ANY)


def gelu(t):
    half = 0.5 * t
    return half + half * jnp.tanh(t * (0.7978845608 + (0.7978845608 * 0.044715) * (t * t)))


def pair_weight(block, blank, count):
    return jnp.concatenate(
        [
            jnp.concatenate([block(k, b) if k < 3 else blank, block(k - 1, b) if k > 0 else blank], axis=1)
            for k in range(4)
            for b in range(count)
        ],
        axis=0,
    )


def spatial_weight(weight_ref, layer):
    blank = jnp.zeros(weight_ref.shape[-2:], weight_ref.dtype)
    return pair_weight(lambda k, b: weight_ref[layer, k, b], blank, 3)


def put_shifted(dst, row, cells):
    groups, width, chans = cells.shape
    for shift, moved in ((0, pltpu.roll(cells, 1, 1)), (1, cells), (2, pltpu.roll(cells, width - 1, 1))):
        dst[shift, row] = moved.reshape(groups * width, chans).astype(dst.dtype)


def clear_borders(buf):
    for shift in range(3):
        for row in (0, buf.shape[1] - 1):
            buf[shift, row] = jnp.zeros(buf.shape[2:], buf.dtype)


def pack_kernel(
    side_ref, lead_ref, field_hbm, weight_hbm, spatial_hbm, angular_hbm,
    near_ref, far_ref, spatial_ref, angular_ref, mid_ref, edge_ref, saved_ref,
    tiles, field, weight, even, odd, sems,
):
    cols = field_hbm.shape[2]
    copies = [
        pltpu.make_async_copy(field_hbm.at[:, :, pl.ds(start, TILE)], tiles.at[i], sems.at[i])
        for i, start in enumerate((0, cols - TILE))
    ]
    copies.append(pltpu.make_async_copy(spatial_hbm, spatial_ref, sems.at[2]))
    copies.append(pltpu.make_async_copy(angular_hbm, angular_ref, sems.at[3]))
    for copy in copies:
        copy.start()
    for copy in copies:
        copy.wait()
    first = side_ref[0] == 0
    for view in range(tiles.shape[1]):
        head = tiles[0, view].astype(jnp.float32)[:, :EDGE]
        tail = tiles[1, view].astype(jnp.float32)[:, TILE - EDGE :]
        near_ref[view] = jnp.where(first, tail, head).astype(near_ref.dtype)
        far_ref[view] = jnp.where(first, head, tail).astype(far_ref.dtype)

    @pl.when(lead_ref[0] == 0)
    def _():
        loads = (
            pltpu.make_async_copy(field_hbm, field, sems.at[0]),
            pltpu.make_async_copy(weight_hbm, weight, sems.at[1]),
        )
        for load in loads:
            load.start()
        for load in loads:
            load.wait()
        inner_layers(field, weight, spatial_ref, mid_ref, edge_ref, saved_ref, even, odd)


def inner_kernel(
    lead_ref, field_ref, weight_ref, offset_ref, mid_in, edge_in, saved_in,
    mid_ref, edge_ref, saved_ref, even, odd,
):
    @pl.when(lead_ref[0] == 0)
    def _():
        mid_ref[...] = mid_in[...]
        edge_ref[...] = edge_in[...]
        saved_ref[...] = saved_in[...]

    @pl.when(lead_ref[0] != 0)
    def _():
        inner_layers(field_ref, weight_ref, offset_ref, mid_ref, edge_ref, saved_ref, even, odd)


def inner_layers(field_ref, weight_ref, offset_ref, mid_ref, edge_ref, saved_ref, even, odd):
    views, rows, cols, chans = field_ref.shape
    layers = weight_ref.shape[0]
    mid = cols - TILE
    bufs = (even, odd)
    for buf in bufs:
        clear_borders(buf)

    def keep(layer, row, cells):
        saved_ref[layer, row] = cells[:, mid:].reshape(views * TILE, chans).astype(saved_ref.dtype)

    for row in range(rows):
        cells = pltpu.roll(field_ref[:, row].astype(jnp.float32), cols - EDGE, 1)
        put_shifted(even, row + 1, cells)
        keep(0, row, cells)
    for layer in range(layers):
        src, dst = bufs[layer % 2], bufs[(layer + 1) % 2]
        weight = spatial_weight(weight_ref, layer)
        offset = offset_ref[layer : layer + 1]
        for pair in range(rows // 2):
            stacked = jnp.concatenate([src[b, 2 * pair + k] for k in range(4) for b in range(3)], axis=1)
            total = jnp.dot(stacked, weight, preferred_element_type=jnp.float32)
            cells = [
                gelu(total[:, r * chans : (r + 1) * chans] + offset).reshape(views, cols, chans) for r in range(2)
            ]
            if layer == layers - 1:
                part = pl.ds(2 * mid * pair, 2 * mid)
                mid_ref[:, part] = jnp.concatenate([c[:, :mid] for c in cells], axis=1).astype(mid_ref.dtype)
                part = pl.ds(2 * TILE * pair, 2 * TILE)
                edge_ref[:, part] = jnp.concatenate([c[:, mid:] for c in cells], axis=1).astype(edge_ref.dtype)
            else:
                for r in range(2):
                    put_shifted(dst, 2 * pair + r + 1, cells[r])
                    keep(layer + 1, 2 * pair + r, cells[r])


def outer_kernel(
    side_ref, near_ref, far_ref, saved_ref, mid_ref, inner_ref, weight_ref, offset_ref,
    whole_ref, edge_ref, even, odd,
):
    all_views, rows, _, chans = near_ref.shape
    layers = weight_ref.shape[0]
    bufs = (even, odd)
    groups = even.shape[0]
    views = all_views // groups
    mid = mid_ref.shape[1]
    first = side_ref[0] == 0
    place = lax.broadcasted_iota(jnp.int32, (views, TILE, chans), 1)
    whole_ref[:, :mid] = mid_ref[...]

    def kept(layer, row, group):
        part = saved_ref[layer, row, group * views * TILE : (group + 1) * views * TILE]
        return part.astype(jnp.float32).reshape(views, TILE, chans)

    for group in range(groups):
        for buf in bufs:
            clear_borders(buf.at[group])
        span = slice(group * views, (group + 1) * views)
        for row in range(rows):
            near = near_ref[span, row].astype(jnp.float32)
            far = far_ref[span, row].astype(jnp.float32)
            right = jnp.where(first, near, far)
            left = jnp.where(first, far, near)
            own = kept(0, row, group)
            cells = jnp.concatenate([left, own[:, EDGE:], own[:, :EDGE], right], axis=1)
            put_shifted(even.at[group], row + 1, cells)
    for layer in range(layers):
        weight = spatial_weight(weight_ref, layer)
        offset = offset_ref[layer : layer + 1]
        fresh = layer + 1
        for group in range(groups):
            src, dst = bufs[layer % 2].at[group], bufs[(layer + 1) % 2].at[group]
            stacked = jnp.concatenate(
                [
                    jnp.concatenate([src[b, 2 * pair + k] for pair in range(rows // 2)], axis=0)
                    for k in range(4)
                    for b in range(3)
                ],
                axis=1,
            )
            total = jnp.dot(stacked, weight, preferred_element_type=jnp.float32)
            span = views * 2 * TILE
            part = slice(group * views, (group + 1) * views)
            for pair in range(rows // 2):
                ends = []
                for r in range(2):
                    value = gelu(
                        total[pair * span : (pair + 1) * span, r * chans : (r + 1) * chans] + offset
                    ).reshape(views, 2 * TILE, chans)
                    lower, upper = value[:, :TILE], value[:, TILE:]
                    row = 2 * pair + r
                    if layer == layers - 1:
                        ends.append((lower, upper))
                    else:
                        own = kept(fresh, row, group)
                        lower = jnp.where(place >= EDGE + fresh, own, lower)
                        upper = jnp.where(place < EDGE - fresh, own, upper)
                        put_shifted(dst, row + 1, jnp.concatenate([lower, upper], axis=1))
                if ends:
                    own = inner_ref[part, 2 * TILE * pair : 2 * TILE * (pair + 1)].astype(jnp.float32)
                    done = []
                    for r, (lower, upper) in enumerate(ends):
                        tile = own[:, r * TILE : (r + 1) * TILE]
                        tile = jnp.where((place >= EDGE) & (place < EDGE + fresh), lower, tile)
                        done.append(jnp.where((place < EDGE) & (place >= EDGE - fresh), upper, tile))
                    done = jnp.concatenate(done, axis=1).astype(edge_ref.dtype)
                    edge_ref[part, 2 * TILE * pair : 2 * TILE * (pair + 1)] = done
                    whole_ref[part, mid + 2 * TILE * pair : mid + 2 * TILE * (pair + 1)] = done


def view_pair(sources, pair, views, blank):
    stacked, weight = [], []
    for load, taps in sources:
        for k in range(4):
            view = 2 * pair + k - 1
            if 0 <= view < views:
                stacked.append(load(view))
                weight.append(
                    jnp.concatenate([taps(k) if k < 3 else blank, taps(k - 1) if k > 0 else blank], axis=1)
                )
    return jnp.dot(
        jnp.concatenate(stacked, axis=1), jnp.concatenate(weight, axis=0), preferred_element_type=jnp.float32
    )


def partial_kernel(side_ref, hidden_ref, near_ref, weight_ref, offset_ref, out_ref):
    pairs, _, wide = out_ref.shape
    chans = wide // 2
    near_tap = jnp.where(side_ref[0] == 0, 2, 0)
    blank = jnp.zeros((chans, chans), weight_ref.dtype)
    offset = jnp.concatenate([offset_ref[...]] * 2, axis=1)
    sources = (
        (lambda view: hidden_ref[view], lambda k: weight_ref[1, k]),
        (lambda view: near_ref[view], lambda k: weight_ref[near_tap, k]),
    )
    for pair in range(pairs):
        out_ref[pair] = view_pair(sources, pair, 2 * pairs, blank) + offset


def final_kernel(side_ref, mid_ref, edge_ref, partial_ref, weight_ref, field_ref, out_hbm, out, sems):
    views, rows, cols, chans = field_ref.shape
    far_tap = jnp.where(side_ref[0] == 0, 0, 2)
    blank = jnp.zeros((chans, chans), weight_ref.dtype)
    mid = rows * (cols - TILE)
    sources = (
        (lambda view: jnp.concatenate([mid_ref[view], edge_ref[view]], axis=0), lambda k: weight_ref[far_tap, k]),
    )
    copies = []
    for pair in range(views // 2):
        total = view_pair(sources, pair, views, blank) + partial_ref[pair]
        for r in range(2):
            view = 2 * pair + r
            angular = total[:, r * chans : (r + 1) * chans].astype(jnp.bfloat16).astype(jnp.float32)
            cells = jnp.concatenate(
                [angular[:mid].reshape(rows, cols - TILE, chans), angular[mid:].reshape(rows, TILE, chans)], axis=1
            )
            out[view] = (field_ref[view].astype(jnp.float32) + pltpu.roll(cells, EDGE, 1)).astype(out.dtype)
        part = pl.ds(2 * pair, 2)
        copies.append(pltpu.make_async_copy(out.at[part], out_hbm.at[part], sems.at[pair]))
        copies[-1].start()
    for copy in copies:
        copy.wait()


def swap(cells, axis, start, count, closed):
    pairs = []
    for i in range(start, count, 2):
        j = i + 1
        if j < count or closed:
            pairs += [(i, j % count), (j % count, i)]
    return lax.ppermute(cells, axis, pairs)


def params(mebibytes):
    return pltpu.CompilerParams(vmem_limit_bytes=mebibytes * 2**20)


def local(light_field, spatial_weights, spatial_offsets, angular_weight, angular_offset):
    views, rows, cols, chans = light_field.shape
    lon_count, view_count = lax.axis_size("lon"), lax.axis_size("view")
    lead = lax.axis_index("lon")[None]
    lon_side = lax.rem(lax.axis_index("lon"), 2)[None]
    view_side = lax.rem(lax.axis_index("view"), 2)[None]
    layers = spatial_weights.shape[0]
    half = jnp.bfloat16

    def shaped(*shape):
        return jax.ShapeDtypeStruct(shape, half)

    edges = shaped(views, rows, EDGE, chans)
    inner_shapes = (
        shaped(views, rows * (cols - TILE), chans),
        shaped(views, rows * TILE, chans),
        shaped(layers, rows, views * TILE, chans),
    )
    biases = [jax.ShapeDtypeStruct(b.shape, jnp.float32) for b in (spatial_offsets, angular_offset[None])]
    inner_scratch = [pltpu.VMEM((3, rows + 2, views * cols, chans), half)] * 2
    in_hbm = lambda array: pltpu.with_memory_space_constraint(array, pltpu.HBM)
    near, far, spatial_bias, angular_bias, *early = pl.pallas_call(
        pack_kernel,
        out_shape=(edges, edges, *biases, *inner_shapes),
        in_specs=[SMEM, SMEM, HBM, HBM, HBM, HBM],
        out_specs=(VMEM,) * 7,
        scratch_shapes=[
            pltpu.VMEM((2, views, rows, TILE, chans), half),
            pltpu.VMEM(light_field.shape, half),
            pltpu.VMEM(spatial_weights.shape, half),
            *inner_scratch,
            pltpu.SemaphoreType.DMA((4,)),
        ],
        compiler_params=params(20),
        cost_estimate=pl.CostEstimate(flops=2 * 10**9, bytes_accessed=10**7, transcendentals=0),
        name="pack",
    )(lon_side, lead, in_hbm(light_field), in_hbm(spatial_weights), in_hbm(spatial_offsets), in_hbm(angular_offset[None]))
    far = swap(far, "lon", 1, lon_count, True)
    near = swap(near, "lon", 0, lon_count, True)

    mid, edge, saved = pl.pallas_call(
        inner_kernel,
        out_shape=inner_shapes,
        in_specs=[SMEM] + [VMEM] * 6,
        out_specs=(VMEM,) * 3,
        scratch_shapes=inner_scratch,
        compiler_params=params(20),
        name="inner",
    )(lead, light_field, spatial_weights, spatial_bias, *early)
    far_mid = swap(mid, "view", 1, view_count, False)
    whole, edge = pl.pallas_call(
        outer_kernel,
        out_shape=(shaped(views, rows * cols, chans), inner_shapes[1]),
        in_specs=[SMEM] + [VMEM] * 7,
        out_specs=(VMEM, VMEM),
        scratch_shapes=[pltpu.VMEM((GROUPS, 3, rows + 2, views // GROUPS * 2 * TILE, chans), half)] * 2,
        compiler_params=params(16),
        name="outer",
    )(lon_side, near, far, saved, mid, edge, spatial_weights, spatial_bias)
    far_edge = swap(edge, "view", 1, view_count, False)
    near_rows = swap(whole, "view", 0, view_count, False)
    partial = pl.pallas_call(
        partial_kernel,
        out_shape=jax.ShapeDtypeStruct((views // 2, rows * cols, 2 * chans), jnp.float32),
        in_specs=[SMEM] + [VMEM] * 4,
        out_specs=VMEM,
        compiler_params=params(8),
        name="partial",
    )(view_side, whole, near_rows, angular_weight, angular_bias)
    return pl.pallas_call(
        final_kernel,
        out_shape=jax.ShapeDtypeStruct(light_field.shape, half),
        in_specs=[SMEM] + [VMEM] * 5,
        out_specs=HBM,
        scratch_shapes=[
            pltpu.VMEM(light_field.shape, half),
            pltpu.SemaphoreType.DMA((views // 2,)),
        ],
        compiler_params=params(8),
        name="final",
    )(view_side, far_mid, far_edge, partial, angular_weight, light_field)


def solution(mesh):
    return jax.shard_map(
        local,
        mesh=mesh,
        in_specs=(P(("grp", "view"), None, "lon", None), P(), P(), P(), P()),
        out_specs=P(("grp", "view"), None, "lon", None),
        check_vma=False,
    )
```

time: 70.7 us -> 72.7 us (1.028)
  starting transfers between devices: 54 us -> 56.7 us
  local copies, waits for them, and re-layouts: 1.82 us -> 0.01 us
  Pallas kernels: 8.43 us -> 9.91 us
    ppermute x4 -> x5, starting transfers between devices: 54 us -> 56.7 us  [swap(): return lax.ppermute(cells, axis, pairs)]
    unnamed x10 -> x6, local copies, waits for them, and re-layouts: 1.82 us -> 0.01 us
    pallas_call x3, Pallas kernels: 6.58 us -> 8.02 us  [the longest x1 6.01 us: local(): pl.pallas_call(pack_kernel, out_shape=(edges, edges, *biases, *inner_shap...]
    ppermute x4 -> x5, waiting for transfers between devices: 6.03 us -> 5.75 us  [swap(): return lax.ppermute(cells, axis, pairs)]
  transfers between devices with their start and end apart: 4 -> 5, of which waited for: 1 -> 2; matrix products, arithmetic and copies ran while one was open for 0% -> 0% of each run, Pallas kernels for 6% -> 1%
where the time goes in v3:
time: 72.7 us; the launch traced here: 72.5 us
  starting transfers between devices  56.7 us (78%)
  Pallas kernels  9.91 us (14%)
  waiting for transfers between devices  5.75 us (8%)
    ppermute x5, starting transfers between devices, swap(): return lax.ppermute(cells, axis, pairs)  56.7 us
    pallas_call x1, Pallas kernels, local(): pl.pallas_call(pack_kernel, out_shape=(edges, edges, *biases, *inner_shap...  6.01 us
    ppermute x5, waiting for transfers between devices, swap(): return lax.ppermute(cells, axis, pairs)  5.75 us
    pallas_call x1, Pallas kernels, local(): pl.pallas_call(outer_kernel, out_shape=(shaped(views, rows * cols, chans)...  1.93 us
  transfers between devices with their start and end apart: 5, of which 2 were waited for; matrix products, arithmetic and copies ran while one was open for 0% of the time, Pallas kernels for 1%

profile of v3, /device:TPU:33, one launch (start us, length us, event | category | flops | bytes accessed | tf_op | source)
XLA Modules:
  0.0 72.5 jit_solution(13537102634787450226)
XLA Ops:
  0.0 0.0 copy-start
  0.0 0.0 copy-start.1
  0.0 6.0 %pack.1 = (bf16[8,8,4,128]{3,2,1,0:T(4,128)(2,1)S(1)}, bf16[8,8,4,128]{3,2,1,0:T(4,128)(2,1)S(1)}, f32[3,128]{1,0:T(4,128)S(1)}, f32[1,128]{1,0:T(1,128)S(1)}, b...) custom-call(s32[1]{0:T(128)} %bitcast.2.side_ref, ...), custom_call_target="tpu_custom_call" | custom-call | flops 2000000000 | bytes 10000000 | tf_op jit(solution)/shard_map/pack/pallas_call | solution.py:299
  6.0 2.0 %collective-permute-start.1 = (bf16[8,8,4,128]{3,2,1,0:T(4,128)(2,1)S(1)}, bf16[8,8,4,128]{3,2,1,0:T(4,128)(2,1)S(1)}, u32[]{:S(2)}, u32[]{:S(2)}) collective-permute-start(bf16[8,8,4,128]{3,2,1,0:T(4,128)(2,1)S(1)} %get-tuple-element.22), channel_id=1, source_target_pairs={{0,8},{8,0},{16,24},{24,16},{32,40},{40,32},{48,56},{56,48},{64,72... | collective-permute-start | bytes 196616 | tf_op jit(solution)/shard_map/ppermute | solution.py:271
  8.0 41.1 %collective-permute-start.2 = (bf16[8,8,4,128]{3,2,1,0:T(4,128)(2,1)S(1)}, bf16[8,8,4,128]{3,2,1,0:T(4,128)(2,1)S(1)}, u32[]{:S(2)}, u32[]{:S(2)}) collective-permute-start(bf16[8,8,4,128]{3,2,1,0:T(4,128)(2,1)S(1)} %get-tuple-element.23), channel_id=1, source_target_pairs={{8,16},{16,8},{24,32},{32,24},{40,48},{48,40},{56,64},{64,56},{72,... | collective-permute-start | bytes 196616 | tf_op jit(solution)/shard_map/ppermute | solution.py:271
  49.1 0.0 copy-done
  49.1 0.0 copy-done.1
  49.1 0.1 inner.1
  49.2 0.0 collective-permute-done.1.near_ref
  49.2 1.5 %collective-permute-done.2.far_ref = bf16[8,8,4,128]{3,2,1,0:T(4,128)(2,1)S(1)} collective-permute-done((bf16[8,8,4,128]{3,2,1,0:T(4,128)(2,1)S(1)}, bf16[8,8,4,128]{3,2,1,0:T(4,128)(2,1)S(1)}, u32[]{:S(2)}, u32[]{:S(2)}) %collective-permute-start.2) | collective-permute-done | bytes 65568 | tf_op jit(solution)/shard_map/ppermute | solution.py:271
  50.7 0.0 copy-start.2
  50.7 1.9 %outer.1 = (bf16[8,256,128]{2,1,0:T(8,128)(2,1)S(1)}, bf16[8,64,128]{2,1,0:T(8,128)(2,1)S(1)}) custom-call(s32[1]{0:T(128)} %bitcast.2.side_ref, bf16[8,8,4,128]{3,2,1,0:T(4,128)(2,1)S(1)} %collective-permute-done.1.near_ref, bf16[8,8,4,128]{3,2,1,0:T(4,128)(2,1)S(1)} %collective-permute-done.2.far_ref, ...), custom_call_target="tpu_custom_call" | custom-call | tf_op jit(solution)/shard_map/outer/pallas_call | solution.py:328
  52.6 8.0 %collective-permute-start.4 = (bf16[8,256,128]{2,1,0:T(8,128)(2,1)S(1)}, bf16[8,256,128]{2,1,0:T(8,128)(2,1)S(1)}, u32[]{:S(2)}, u32[]{:S(2)}) collective-permute-start(bf16[8,256,128]{2,1,0:T(8,128)(2,1)S(1)} %get-tuple-element.27.hidden_ref), channel_id=1, source_target_pairs={{0,1},{1,0},{2,3},{3,2},{4,5},{5,4},{6,7},{7,6},{8,9},{9,8},{10,11... | collective-permute-start | bytes 1572872 | tf_op jit(solution)/shard_map/ppermute | solution.py:271
  60.7 2.0 %collective-permute-start = (bf16[8,192,128]{2,1,0:T(8,128)(2,1)S(1)}, bf16[8,192,128]{2,1,0:T(8,128)(2,1)S(1)}, u32[]{:S(2)}, u32[]{:S(2)}) collective-permute-start(bf16[8,192,128]{2,1,0:T(8,128)(2,1)S(1)} %get-tuple-element.21.mid_ref), channel_id=1, source_target_pairs={{1,2},{2,1},{3,4},{4,3},{5,6},{6,5},{9,10},{10,9},{11,12},{12,11},... | collective-permute-start | bytes 1179656 | tf_op jit(solution)/shard_map/ppermute | solution.py:271
  62.7 3.7 %collective-permute-start.3 = (bf16[8,64,128]{2,1,0:T(8,128)(2,1)S(1)}, bf16[8,64,128]{2,1,0:T(8,128)(2,1)S(1)}, u32[]{:S(2)}, u32[]{:S(2)}) collective-permute-start(bf16[8,64,128]{2,1,0:T(8,128)(2,1)S(1)} %get-tuple-element.26), channel_id=1, source_target_pairs={{1,2},{2,1},{3,4},{4,3},{5,6},{6,5},{9,10},{10,9},{11,12},{12,11},... | collective-permute-start | bytes 393224 | tf_op jit(solution)/shard_map/ppermute | solution.py:271
  66.3 0.0 collective-permute-done.4.near_ref
  66.4 0.0 copy-done.2
  66.4 0.6 partial.1.partial_ref
  67.0 4.2 %collective-permute-done.3.edge_ref = bf16[8,64,128]{2,1,0:T(8,128)(2,1)S(1)} collective-permute-done((bf16[8,64,128]{2,1,0:T(8,128)(2,1)S(1)}, bf16[8,64,128]{2,1,0:T(8,128)(2,1)S(1)}, u32[]{:S(2)}, u32[]{:S(2)}) %collective-permute-start.3) | collective-permute-done | bytes 131104 | tf_op jit(solution)/shard_map/ppermute | solution.py:271
  71.2 0.0 collective-permute-done.mid_ref
  71.2 1.3 %final.1 = bf16[8,8,32,128]{3,2,1,0:T(8,128)(2,1)} custom-call(s32[1]{0:T(128)} %bitcast.side_ref, bf16[8,192,128]{2,1,0:T(8,128)(2,1)S(1)} %collective-permute-done.mid_ref, bf16[8,64,128]{2,1,0:T(8,128)(2,1)S(1)} %collective-permute-done.3.edge_ref, f32[4,256,256]{2,1,0:T(8,128)S(1)} %partial.1.partial_ref, bf16[3,3,128,128]{3,2,1,0:T(8,128)(2,1)S(1)} %copy-done.2, ...), custom_call_target="tpu_custom_call" | custom-call | tf_op jit(solution)/shard_map/final/pallas_call | solution.py:347
Async XLA Ops:
  0.0 49.1 %copy-start = (bf16[3,3,3,128,128]{4,3,2,1,0:T(8,128)(2,1)S(1)}, bf16[3,3,3,128,128]{4,3,2,1,0:T(8,128)(2,1)}, u32[]{:S(2)}) copy-start(bf16[3,3,3,128,128]{4,3,2,1,0:T(8,128)(2,1)} %weight_ref.5) | copy-start | bytes 2654212
  0.0 49.1 %copy-start.1 = (bf16[8,8,32,128]{3,2,1,0:T(8,128)(2,1)S(1)}, bf16[8,8,32,128]{3,2,1,0:T(8,128)(2,1)}, u32[]{:S(2)}) copy-start(bf16[8,8,32,128]{3,2,1,0:T(8,128)(2,1)} %field_ref.3) | copy-start | bytes 1572868
  6.0 43.1 %collective-permute-start.1 = (bf16[8,8,4,128]{3,2,1,0:T(4,128)(2,1)S(1)}, bf16[8,8,4,128]{3,2,1,0:T(4,128)(2,1)S(1)}, u32[]{:S(2)}, u32[]{:S(2)}) collective-permute-start(bf16[8,8,4,128]{3,2,1,0:T(4,128)(2,1)S(1)} %get-tuple-element.22), channel_id=1, source_target_pairs={{0,8},{8,0},{16,24},{24,16},{32,40},{40,32},{48,56},{56,48},{64,72... | collective-permute-start | bytes 196616 | tf_op jit(solution)/shard_map/ppermute | solution.py:271
  8.0 42.7 %collective-permute-start.2 = (bf16[8,8,4,128]{3,2,1,0:T(4,128)(2,1)S(1)}, bf16[8,8,4,128]{3,2,1,0:T(4,128)(2,1)S(1)}, u32[]{:S(2)}, u32[]{:S(2)}) collective-permute-start(bf16[8,8,4,128]{3,2,1,0:T(4,128)(2,1)S(1)} %get-tuple-element.23), channel_id=1, source_target_pairs={{8,16},{16,8},{24,32},{32,24},{40,48},{48,40},{56,64},{64,56},{72,... | collective-permute-start | bytes 196616 | tf_op jit(solution)/shard_map/ppermute | solution.py:271
  50.7 15.7 %copy-start.2 = (bf16[3,3,128,128]{3,2,1,0:T(8,128)(2,1)S(1)}, bf16[3,3,128,128]{3,2,1,0:T(8,128)(2,1)}, u32[]{:S(2)}) copy-start(bf16[3,3,128,128]{3,2,1,0:T(8,128)(2,1)} %weight_ref.7) | copy-start | bytes 884740
  52.6 13.7 %collective-permute-start.4 = (bf16[8,256,128]{2,1,0:T(8,128)(2,1)S(1)}, bf16[8,256,128]{2,1,0:T(8,128)(2,1)S(1)}, u32[]{:S(2)}, u32[]{:S(2)}) collective-permute-start(bf16[8,256,128]{2,1,0:T(8,128)(2,1)S(1)} %get-tuple-element.27.hidden_ref), channel_id=1, source_target_pairs={{0,1},{1,0},{2,3},{3,2},{4,5},{5,4},{6,7},{7,6},{8,9},{9,8},{10,11... | collective-permute-start | bytes 1572872 | tf_op jit(solution)/shard_map/ppermute | solution.py:271
  60.7 10.5 %collective-permute-start = (bf16[8,192,128]{2,1,0:T(8,128)(2,1)S(1)}, bf16[8,192,128]{2,1,0:T(8,128)(2,1)S(1)}, u32[]{:S(2)}, u32[]{:S(2)}) collective-permute-start(bf16[8,192,128]{2,1,0:T(8,128)(2,1)S(1)} %get-tuple-element.21.mid_ref), channel_id=1, source_target_pairs={{1,2},{2,1},{3,4},{4,3},{5,6},{6,5},{9,10},{10,9},{11,12},{12,11},... | collective-permute-start | bytes 1179656 | tf_op jit(solution)/shard_map/ppermute | solution.py:271
  62.7 8.6 %collective-permute-start.3 = (bf16[8,64,128]{2,1,0:T(8,128)(2,1)S(1)}, bf16[8,64,128]{2,1,0:T(8,128)(2,1)S(1)}, u32[]{:S(2)}, u32[]{:S(2)}) collective-permute-start(bf16[8,64,128]{2,1,0:T(8,128)(2,1)S(1)} %get-tuple-element.26), channel_id=1, source_target_pairs={{1,2},{2,1},{3,4},{4,3},{5,6},{6,5},{9,10},{10,9},{11,12},{12,11},... | collective-permute-start | bytes 393224 | tf_op jit(solution)/shard_map/ppermute | solution.py:271

commit v4 on v3

--- a/solution.py
+++ b/solution.py
@@ -70,7 +70,7 @@
         near_ref[view] = jnp.where(first, tail, head).astype(near_ref.dtype)
         far_ref[view] = jnp.where(first, head, tail).astype(far_ref.dtype)
 
-    @pl.when(lead_ref[0] == 0)
+    @pl.when(lead_ref[0] != 0)
     def _():
         loads = (
             pltpu.make_async_copy(field_hbm, field, sems.at[0]),
@@ -87,13 +87,13 @@
     lead_ref, field_ref, weight_ref, offset_ref, mid_in, edge_in, saved_in,
     mid_ref, edge_ref, saved_ref, even, odd,
 ):
-    @pl.when(lead_ref[0] == 0)
+    @pl.when(lead_ref[0] != 0)
     def _():
         mid_ref[...] = mid_in[...]
         edge_ref[...] = edge_in[...]
         saved_ref[...] = saved_in[...]
 
-    @pl.when(lead_ref[0] != 0)
+    @pl.when(lead_ref[0] == 0)
     def _():
         inner_layers(field_ref, weight_ref, offset_ref, mid_ref, edge_ref, saved_ref, even, odd)
 
@@ -135,7 +135,7 @@
 
 
 def outer_kernel(
-    side_ref, near_ref, far_ref, saved_ref, mid_ref, inner_ref, weight_ref, offset_ref,
+    side_ref, near_ref, rest_ref, far_ref, saved_ref, mid_ref, inner_ref, weight_ref, offset_ref,
     whole_ref, edge_ref, even, odd,
 ):
     all_views, rows, _, chans = near_ref.shape
@@ -157,7 +157,7 @@
             clear_borders(buf.at[group])
         span = slice(group * views, (group + 1) * views)
         for row in range(rows):
-            near = near_ref[span, row].astype(jnp.float32)
+            near = near_ref[span, row].astype(jnp.float32) + rest_ref[span, row].astype(jnp.float32)
             far = far_ref[span, row].astype(jnp.float32)
             right = jnp.where(first, near, far)
             left = jnp.where(first, far, near)
@@ -223,28 +223,29 @@
     )
 
 
-def partial_kernel(side_ref, hidden_ref, near_ref, weight_ref, offset_ref, out_ref):
+def partial_kernel(side_ref, hidden_ref, lead_ref, rest_ref, edge_ref, weight_ref, offset_ref, out_ref):
     pairs, _, wide = out_ref.shape
     chans = wide // 2
-    near_tap = jnp.where(side_ref[0] == 0, 2, 0)
+    far_tap = jnp.where(side_ref[0] == 0, 0, 2)
     blank = jnp.zeros((chans, chans), weight_ref.dtype)
     offset = jnp.concatenate([offset_ref[...]] * 2, axis=1)
     sources = (
         (lambda view: hidden_ref[view], lambda k: weight_ref[1, k]),
-        (lambda view: near_ref[view], lambda k: weight_ref[near_tap, k]),
+        (
+            lambda view: jnp.concatenate([lead_ref[view] + rest_ref[view], edge_ref[view]], axis=0),
+            lambda k: weight_ref[far_tap, k],
+        ),
     )
     for pair in range(pairs):
         out_ref[pair] = view_pair(sources, pair, 2 * pairs, blank) + offset
 
 
-def final_kernel(side_ref, mid_ref, edge_ref, partial_ref, weight_ref, field_ref, out_hbm, out, sems):
+def final_kernel(side_ref, near_ref, partial_ref, weight_ref, field_ref, out_hbm, out, sems):
     views, rows, cols, chans = field_ref.shape
-    far_tap = jnp.where(side_ref[0] == 0, 0, 2)
+    near_tap = jnp.where(side_ref[0] == 0, 2, 0)
     blank = jnp.zeros((chans, chans), weight_ref.dtype)
     mid = rows * (cols - TILE)
-    sources = (
-        (lambda view: jnp.concatenate([mid_ref[view], edge_ref[view]], axis=0), lambda k: weight_ref[far_tap, k]),
-    )
+    sources = ((lambda view: near_ref[view], lambda k: weight_ref[near_tap, k]),)
     copies = []
     for pair in range(views // 2):
         total = view_pair(sources, pair, views, blank) + partial_ref[pair]
@@ -262,13 +263,12 @@
         copy.wait()
 
 
-def swap(cells, axis, start, count, closed):
+def neighbours(starts, count, closed=False):
     pairs = []
-    for i in range(start, count, 2):
-        j = i + 1
-        if j < count or closed:
-            pairs += [(i, j % count), (j % count, i)]
-    return lax.ppermute(cells, axis, pairs)
+    for i in starts:
+        if i + 1 < count or closed:
+            pairs += [(i, (i + 1) % count), ((i + 1) % count, i)]
+    return pairs
 
 
 def params(mebibytes):
@@ -278,9 +278,9 @@
 def local(light_field, spatial_weights, spatial_offsets, angular_weight, angular_offset):
     views, rows, cols, chans = light_field.shape
     lon_count, view_count = lax.axis_size("lon"), lax.axis_size("view")
-    lead = lax.axis_index("lon")[None]
-    lon_side = lax.rem(lax.axis_index("lon"), 2)[None]
-    view_side = lax.rem(lax.axis_index("view"), 2)[None]
+    lon, view = lax.axis_index("lon"), lax.axis_index("view")
+    lead = ((lon == 0) & (view > 0) & (view < view_count - 1)).astype(jnp.int32)[None]
+    lon_side, view_side = lax.rem(lon, 2)[None], lax.rem(view, 2)[None]
     layers = spatial_weights.shape[0]
     half = jnp.bfloat16
 
@@ -308,12 +308,18 @@
             *inner_scratch,
             pltpu.SemaphoreType.DMA((4,)),
         ],
-        compiler_params=params(20),
+        compiler_params=params(12),
         cost_estimate=pl.CostEstimate(flops=2 * 10**9, bytes_accessed=10**7, transcendentals=0),
         name="pack",
     )(lon_side, lead, in_hbm(light_field), in_hbm(spatial_weights), in_hbm(spatial_offsets), in_hbm(angular_offset[None]))
-    far = swap(far, "lon", 1, lon_count, True)
-    near = swap(near, "lon", 0, lon_count, True)
+    far_views = neighbours(range(1, view_count, 2), view_count)
+    rest_views = [
+        (line * view_count + i, line * view_count + j) for line in range(1, lon_count) for i, j in far_views
+    ]
+    near_lead = lax.ppermute(near, "lon", neighbours(range(0, 2, 2), lon_count))
+    mid_lead = lax.ppermute(early[0], ("lon", "view"), far_views)
+    far = lax.ppermute(far, "lon", neighbours(range(1, lon_count, 2), lon_count, True))
+    near_rest = lax.ppermute(near, "lon", neighbours(range(2, lon_count, 2), lon_count))
 
     mid, edge, saved = pl.pallas_call(
         inner_kernel,
@@ -321,41 +327,41 @@
         in_specs=[SMEM] + [VMEM] * 6,
         out_specs=(VMEM,) * 3,
         scratch_shapes=inner_scratch,
-        compiler_params=params(20),
+        compiler_params=params(12),
         name="inner",
     )(lead, light_field, spatial_weights, spatial_bias, *early)
-    far_mid = swap(mid, "view", 1, view_count, False)
+    mid_rest = lax.ppermute(mid, ("lon", "view"), rest_views)
     whole, edge = pl.pallas_call(
         outer_kernel,
         out_shape=(shaped(views, rows * cols, chans), inner_shapes[1]),
-        in_specs=[SMEM] + [VMEM] * 7,
+        in_specs=[SMEM] + [VMEM] * 8,
         out_specs=(VMEM, VMEM),
         scratch_shapes=[pltpu.VMEM((GROUPS, 3, rows + 2, views // GROUPS * 2 * TILE, chans), half)] * 2,
-        compiler_params=params(16),
+        compiler_params=params(6),
         name="outer",
-    )(lon_side, near, far, saved, mid, edge, spatial_weights, spatial_bias)
-    far_edge = swap(edge, "view", 1, view_count, False)
-    near_rows = swap(whole, "view", 0, view_count, False)
+    )(lon_side, near_lead, near_rest, far, saved, mid, edge, spatial_weights, spatial_bias)
+    far_edge = lax.ppermute(edge, "view", far_views)
+    near_rows = lax.ppermute(whole, "view", neighbours(range(0, view_count, 2), view_count))
     partial = pl.pallas_call(
         partial_kernel,
         out_shape=jax.ShapeDtypeStruct((views // 2, rows * cols, 2 * chans), jnp.float32),
-        in_specs=[SMEM] + [VMEM] * 4,
+        in_specs=[SMEM] + [VMEM] * 6,
         out_specs=VMEM,
-        compiler_params=params(8),
+        compiler_params=params(6),
         name="partial",
-    )(view_side, whole, near_rows, angular_weight, angular_bias)
+    )(view_side, whole, mid_lead, mid_rest, far_edge, angular_weight, angular_bias)
     return pl.pallas_call(
         final_kernel,
         out_shape=jax.ShapeDtypeStruct(light_field.shape, half),
-        in_specs=[SMEM] + [VMEM] * 5,
+        in_specs=[SMEM] + [VMEM] * 4,
         out_specs=HBM,
         scratch_shapes=[
             pltpu.VMEM(light_field.shape, half),
             pltpu.SemaphoreType.DMA((views // 2,)),
         ],
-        compiler_params=params(8),
+        compiler_params=params(6),
         name="final",
-    )(view_side, far_mid, far_edge, partial, angular_weight, light_field)
+    )(view_side, near_rows, partial, angular_weight, light_field)
 
 
 def solution(mesh):

time: 72.7 us -> 73.2 us (level)
  starting transfers between devices: 56.7 us -> 54 us
  Pallas kernels: 9.91 us -> 11.5 us
  waiting for transfers between devices: 5.75 us -> 7.27 us
    ppermute x5 -> x7, starting transfers between devices: 56.7 us -> 54 us  [the longest x1 41.1 us: local(): lax.ppermute(far, 'lon', neighbours(range(1, lon_count, 2), lon_count, Tr...]
    ppermute x5 -> x7, waiting for transfers between devices: 5.75 us -> 7.27 us  [the longest x1 4.3 us: local(): far_edge = lax.ppermute(edge, 'view', far_views)]
    pallas_call x1, Pallas kernels: 0.64 us -> 1.55 us  [local(): pl.pallas_call(partial_kernel, out_shape=jax.ShapeDtypeStruct((views // 2...]
  transfers between devices with their start and end apart: 5 -> 7, of which waited for: 2 -> 2; matrix products, arithmetic and copies ran while one was open for 0% -> 0% of each run, Pallas kernels for 1% -> 2%
where the time goes in v4:
time: 73.2 us; the launch traced here: 72.9 us
  starting transfers between devices  54 us (74%)
  Pallas kernels  11.5 us (16%)
  waiting for transfers between devices  7.27 us (10%)
    ppermute x1, starting transfers between devices, local(): lax.ppermute(far, 'lon', neighbours(range(1, lon_count, 2), lon_count, Tr...  41.1 us
    pallas_call x1, Pallas kernels, local(): pl.pallas_call(pack_kernel, out_shape=(edges, edges, *biases, *inner_shap...  6.02 us
    ppermute x1, waiting for transfers between devices, local(): far_edge = lax.ppermute(edge, 'view', far_views)  4.3 us
    ppermute x1, starting transfers between devices, local(): lax.ppermute(whole, 'view', neighbours(range(0, view_count, 2), view_count))  3.96 us
    ppermute x1, starting transfers between devices, local(): mid_lead = lax.ppermute(early[0], ('lon', 'view'), far_views)  3.19 us
    ppermute x1, waiting for transfers between devices, local(): near_lead = lax.ppermute(near, 'lon', neighbours(range(0, 2, 2), lon_count))  2.96 us
    pallas_call x1, Pallas kernels, local(): pl.pallas_call(outer_kernel, out_shape=(shaped(views, rows * cols, chans)...  2.63 us
    ppermute x1, starting transfers between devices, local(): far_edge = lax.ppermute(edge, 'view', far_views)  2.44 us
  transfers between devices with their start and end apart: 7, of which 2 were waited for; matrix products, arithmetic and copies ran while one was open for 0% of the time, Pallas kernels for 2%

profile of v4, /device:TPU:33, one launch (start us, length us, event | category | flops | bytes accessed | tf_op | source)
XLA Modules:
  0.0 72.9 jit_solution(636691515358436026)
XLA Ops:
  0.0 0.0 copy-start
  0.0 0.0 copy-start.1
  0.0 6.0 %pack.1 = (bf16[8,8,4,128]{3,2,1,0:T(4,128)(2,1)S(1)}, bf16[8,8,4,128]{3,2,1,0:T(4,128)(2,1)S(1)}, f32[3,128]{1,0:T(4,128)S(1)}, f32[1,128]{1,0:T(1,128)S(1)}, b...) custom-call(s32[1]{0:T(128)} %bitcast.1.side_ref, ...), custom_call_target="tpu_custom_call" | custom-call | flops 2000000000 | bytes 10000000 | tf_op jit(solution)/shard_map/pack/pallas_call | solution.py:299
  6.0 41.1 %collective-permute-start.2 = (bf16[8,8,4,128]{3,2,1,0:T(4,128)(2,1)S(1)}, bf16[8,8,4,128]{3,2,1,0:T(4,128)(2,1)S(1)}, u32[]{:S(2)}, u32[]{:S(2)}) collective-permute-start(bf16[8,8,4,128]{3,2,1,0:T(4,128)(2,1)S(1)} %get-tuple-element.18), channel_id=1, source_target_pairs={{8,16},{16,8},{24,32},{32,24},{40,48},{48,40},{56,64},{64,56},{72,... | collective-permute-start | bytes 196616 | tf_op jit(solution)/shard_map/ppermute | solution.py:321
  47.1 0.7 collective-permute-start.1
  47.8 2.0 %collective-permute-start = (bf16[8,8,4,128]{3,2,1,0:T(4,128)(2,1)S(1)}, bf16[8,8,4,128]{3,2,1,0:T(4,128)(2,1)S(1)}, u32[]{:S(2)}, u32[]{:S(2)}) collective-permute-start(bf16[8,8,4,128]{3,2,1,0:T(4,128)(2,1)S(1)} %get-tuple-element.17), channel_id=1, source_target_pairs={{0,8},{8,0},{1,9},{9,1},{2,10},{10,2},{3,11},{11,3},{4,12},{12,4},... | collective-permute-start | bytes 196616 | tf_op jit(solution)/shard_map/ppermute | solution.py:319
  49.7 0.0 copy-done
  49.7 0.0 copy-done.1
  49.8 0.1 inner.1
  49.8 0.0 collective-permute-done.2.far_ref
  49.8 0.0 collective-permute-done.1.rest_ref
  49.9 3.0 %collective-permute-done.near_ref = bf16[8,8,4,128]{3,2,1,0:T(4,128)(2,1)S(1)} collective-permute-done((bf16[8,8,4,128]{3,2,1,0:T(4,128)(2,1)S(1)}, bf16[8,8,4,128]{3,2,1,0:T(4,128)(2,1)S(1)}, u32[]{:S(2)}, u32[]{:S(2)}) %collective-permute-start) | collective-permute-done | bytes 65568 | tf_op jit(solution)/shard_map/ppermute | solution.py:319
  52.8 0.0 copy-start.2
  52.8 2.6 %outer.1 = (bf16[8,256,128]{2,1,0:T(8,128)(2,1)S(1)}, bf16[8,64,128]{2,1,0:T(8,128)(2,1)}) custom-call(s32[1]{0:T(128)} %bitcast.1.side_ref, bf16[8,8,4,128]{3,2,1,0:T(4,128)(2,1)S(1)} %collective-permute-done.near_ref, bf16[8,8,4,128]{3,2,1,0:T(4,128)(2,1)S(1)} %collective-permute-done.1.rest_ref, ...), custom_call_target="tpu_custom_call" | custom-call | tf_op jit(solution)/shard_map/outer/pallas_call | solution.py:334
  55.4 4.0 %collective-permute-start.3 = (bf16[8,256,128]{2,1,0:T(8,128)(2,1)S(1)}, bf16[8,256,128]{2,1,0:T(8,128)(2,1)S(1)}, u32[]{:S(2)}, u32[]{:S(2)}) collective-permute-start(bf16[8,256,128]{2,1,0:T(8,128)(2,1)S(1)} %get-tuple-element.26.hidden_ref), channel_id=1, source_target_pairs={{0,1},{1,0},{2,3},{3,2},{4,5},{5,4},{6,7},{7,6},{8,9},{9,8},{10,11... | collective-permute-start | bytes 1572872 | tf_op jit(solution)/shard_map/ppermute | solution.py:344
  59.4 3.2 %collective-permute-start.4 = (bf16[8,192,128]{2,1,0:T(8,128)(2,1)S(1)}, bf16[8,192,128]{2,1,0:T(8,128)(2,1)S(1)}, u32[]{:S(2)}, u32[]{:S(2)}) collective-permute-start(bf16[8,192,128]{2,1,0:T(8,128)(2,1)S(1)} %get-tuple-element.20.mid_in), channel_id=1, source_target_pairs={{1,2},{2,1},{3,4},{4,3},{5,6},{6,5},{257,258},{258,257},{259,260},... | collective-permute-start | bytes 1179656 | tf_op jit(solution)/shard_map/ppermute | solution.py:320
  62.6 0.7 collective-permute-start.5
  63.3 2.4 %collective-permute-start.6 = (bf16[8,64,128]{2,1,0:T(8,128)(2,1)}, bf16[8,64,128]{2,1,0:T(8,128)(2,1)}, u32[]{:S(2)}, u32[]{:S(2)}) collective-permute-start(bf16[8,64,128]{2,1,0:T(8,128)(2,1)} %get-tuple-element.27), channel_id=1, source_target_pairs={{1,2},{2,1},{3,4},{4,3},{5,6},{6,5},{9,10},{10,9},{11,12},{12,11},... | collective-permute-start | bytes 393224 | tf_op jit(solution)/shard_map/ppermute | solution.py:343
  65.7 4.3 %collective-permute-done.6.edge_ref = bf16[8,64,128]{2,1,0:T(8,128)(2,1)} collective-permute-done((bf16[8,64,128]{2,1,0:T(8,128)(2,1)}, bf16[8,64,128]{2,1,0:T(8,128)(2,1)}, u32[]{:S(2)}, u32[]{:S(2)}) %collective-permute-start.6) | collective-permute-done | bytes 131104 | tf_op jit(solution)/shard_map/ppermute | solution.py:343
  70.0 0.0 collective-permute-done.4.lead_ref
  70.1 0.0 collective-permute-done.5.rest_ref
  70.1 0.0 copy-done.2
  70.1 1.5 %partial.1.partial_ref = f32[4,256,256]{2,1,0:T(8,128)S(1)} custom-call(s32[1]{0:T(128)} %bitcast.side_ref, bf16[8,256,128]{2,1,0:T(8,128)(2,1)S(1)} %get-tuple-element.26.hidden_ref, bf16[8,192,128]{2,1,0:T(8,128)(2,1)S(1)} %collective-permute-done.4.lead_ref, bf16[8,192,128]{2,1,0:T(8,128)(2,1)S(1)} %collective-permute-done.5.rest_ref, ...), custom_call_target="tpu_custom_call" | custom-call | tf_op jit(solution)/shard_map/partial/pallas_call | solution.py:345
  71.6 0.0 collective-permute-done.3.near_ref
  71.6 1.3 %final.1 = bf16[8,8,32,128]{3,2,1,0:T(8,128)(2,1)} custom-call(s32[1]{0:T(128)} %bitcast.side_ref, bf16[8,256,128]{2,1,0:T(8,128)(2,1)S(1)} %collective-permute-done.3.near_ref, f32[4,256,256]{2,1,0:T(8,128)S(1)} %partial.1.partial_ref, bf16[3,3,128,128]{3,2,1,0:T(8,128)(2,1)S(1)} %copy-done.2, bf16[8,8,32,128]{3,2,1,0:T(8,128)(2,1)S(1)} %copy-done.1), custom_call_target="tpu_custom_call" | custom-call | tf_op jit(solution)/shard_map/final/pallas_call | solution.py:353
Async XLA Ops:
  0.0 49.7 %copy-start = (bf16[3,3,3,128,128]{4,3,2,1,0:T(8,128)(2,1)S(1)}, bf16[3,3,3,128,128]{4,3,2,1,0:T(8,128)(2,1)}, u32[]{:S(2)}) copy-start(bf16[3,3,3,128,128]{4,3,2,1,0:T(8,128)(2,1)} %weight_ref.5) | copy-start | bytes 2654212
  0.0 49.7 %copy-start.1 = (bf16[8,8,32,128]{3,2,1,0:T(8,128)(2,1)S(1)}, bf16[8,8,32,128]{3,2,1,0:T(8,128)(2,1)}, u32[]{:S(2)}) copy-start(bf16[8,8,32,128]{3,2,1,0:T(8,128)(2,1)} %field_ref.3) | copy-start | bytes 1572868
  6.0 43.8 %collective-permute-start.2 = (bf16[8,8,4,128]{3,2,1,0:T(4,128)(2,1)S(1)}, bf16[8,8,4,128]{3,2,1,0:T(4,128)(2,1)S(1)}, u32[]{:S(2)}, u32[]{:S(2)}) collective-permute-start(bf16[8,8,4,128]{3,2,1,0:T(4,128)(2,1)S(1)} %get-tuple-element.18), channel_id=1, source_target_pairs={{8,16},{16,8},{24,32},{32,24},{40,48},{48,40},{56,64},{64,56},{72,... | collective-permute-start | bytes 196616 | tf_op jit(solution)/shard_map/ppermute | solution.py:321
  47.1 2.7 %collective-permute-start.1 = (bf16[8,8,4,128]{3,2,1,0:T(4,128)(2,1)S(1)}, bf16[8,8,4,128]{3,2,1,0:T(4,128)(2,1)S(1)}, u32[]{:S(2)}, u32[]{:S(2)}) collective-permute-start(bf16[8,8,4,128]{3,2,1,0:T(4,128)(2,1)S(1)} %get-tuple-element.17), channel_id=1, source_target_pairs={{16,24},{24,16},{32,40},{40,32},{48,56},{56,48},{64,72},{72,64},{8... | collective-permute-start | bytes 196616 | tf_op jit(solution)/shard_map/ppermute | solution.py:322
  47.8 5.0 %collective-permute-start = (bf16[8,8,4,128]{3,2,1,0:T(4,128)(2,1)S(1)}, bf16[8,8,4,128]{3,2,1,0:T(4,128)(2,1)S(1)}, u32[]{:S(2)}, u32[]{:S(2)}) collective-permute-start(bf16[8,8,4,128]{3,2,1,0:T(4,128)(2,1)S(1)} %get-tuple-element.17), channel_id=1, source_target_pairs={{0,8},{8,0},{1,9},{9,1},{2,10},{10,2},{3,11},{11,3},{4,12},{12,4},... | collective-permute-start | bytes 196616 | tf_op jit(solution)/shard_map/ppermute | solution.py:319
  52.8 17.2 %copy-start.2 = (bf16[3,3,128,128]{3,2,1,0:T(8,128)(2,1)S(1)}, bf16[3,3,128,128]{3,2,1,0:T(8,128)(2,1)}, u32[]{:S(2)}) copy-start(bf16[3,3,128,128]{3,2,1,0:T(8,128)(2,1)} %weight_ref.7) | copy-start | bytes 884740
  55.4 16.2 %collective-permute-start.3 = (bf16[8,256,128]{2,1,0:T(8,128)(2,1)S(1)}, bf16[8,256,128]{2,1,0:T(8,128)(2,1)S(1)}, u32[]{:S(2)}, u32[]{:S(2)}) collective-permute-start(bf16[8,256,128]{2,1,0:T(8,128)(2,1)S(1)} %get-tuple-element.26.hidden_ref), channel_id=1, source_target_pairs={{0,1},{1,0},{2,3},{3,2},{4,5},{5,4},{6,7},{7,6},{8,9},{9,8},{10,11... | collective-permute-start | bytes 1572872 | tf_op jit(solution)/shard_map/ppermute | solution.py:344
  59.4 10.6 %collective-permute-start.4 = (bf16[8,192,128]{2,1,0:T(8,128)(2,1)S(1)}, bf16[8,192,128]{2,1,0:T(8,128)(2,1)S(1)}, u32[]{:S(2)}, u32[]{:S(2)}) collective-permute-start(bf16[8,192,128]{2,1,0:T(8,128)(2,1)S(1)} %get-tuple-element.20.mid_in), channel_id=1, source_target_pairs={{1,2},{2,1},{3,4},{4,3},{5,6},{6,5},{257,258},{258,257},{259,260},... | collective-permute-start | bytes 1179656 | tf_op jit(solution)/shard_map/ppermute | solution.py:320
  62.6 7.4 %collective-permute-start.5 = (bf16[8,192,128]{2,1,0:T(8,128)(2,1)S(1)}, bf16[8,192,128]{2,1,0:T(8,128)(2,1)S(1)}, u32[]{:S(2)}, u32[]{:S(2)}) collective-permute-start(bf16[8,192,128]{2,1,0:T(8,128)(2,1)S(1)} %get-tuple-element.24.mid_ref), channel_id=1, source_target_pairs={{9,10},{10,9},{11,12},{12,11},{13,14},{14,13},{17,18},{18,17},{19,... | collective-permute-start | bytes 1179656 | tf_op jit(solution)/shard_map/ppermute | solution.py:333
  63.3 6.7 %collective-permute-start.6 = (bf16[8,64,128]{2,1,0:T(8,128)(2,1)}, bf16[8,64,128]{2,1,0:T(8,128)(2,1)}, u32[]{:S(2)}, u32[]{:S(2)}) collective-permute-start(bf16[8,64,128]{2,1,0:T(8,128)(2,1)} %get-tuple-element.27), channel_id=1, source_target_pairs={{1,2},{2,1},{3,4},{4,3},{5,6},{6,5},{9,10},{10,9},{11,12},{12,11},... | collective-permute-start | bytes 393224 | tf_op jit(solution)/shard_map/ppermute | solution.py:343

commit v5 on v4

--- a/solution.py
+++ b/solution.py
@@ -8,7 +8,7 @@
 
 EDGE = 4
 TILE = 8
-GROUPS = 4
+GROUPS = 2
 VMEM = pl.BlockSpec(memory_space=pltpu.VMEM)
 SMEM = pl.BlockSpec(memory_space=pltpu.SMEM)
 HBM = pl.BlockSpec(memory_space=pl.ANY)
@@ -50,9 +50,10 @@
 def pack_kernel(
     side_ref, lead_ref, field_hbm, weight_hbm, spatial_hbm, angular_hbm,
     near_ref, far_ref, spatial_ref, angular_ref, mid_ref, edge_ref, saved_ref,
-    tiles, field, weight, even, odd, sems,
+    tiles, columns, field, weight, even, odd, sems,
 ):
     cols = field_hbm.shape[2]
+    reach, lines, chans = near_ref.shape
     copies = [
         pltpu.make_async_copy(field_hbm.at[:, :, pl.ds(start, TILE)], tiles.at[i], sems.at[i])
         for i, start in enumerate((0, cols - TILE))
@@ -64,11 +65,13 @@
     for copy in copies:
         copy.wait()
     first = side_ref[0] == 0
-    for view in range(tiles.shape[1]):
-        head = tiles[0, view].astype(jnp.float32)[:, :EDGE]
-        tail = tiles[1, view].astype(jnp.float32)[:, TILE - EDGE :]
-        near_ref[view] = jnp.where(first, tail, head).astype(near_ref.dtype)
-        far_ref[view] = jnp.where(first, head, tail).astype(far_ref.dtype)
+    for i in range(2):
+        columns[i] = tiles[i].astype(jnp.float32).reshape(lines * TILE, chans)
+    for c in range(reach):
+        head = columns[0, pl.ds(c, lines, stride=TILE)]
+        tail = columns[1, pl.ds(TILE - reach + c, lines, stride=TILE)]
+        near_ref[c] = jnp.where(first, tail, head).astype(near_ref.dtype)
+        far_ref[c] = jnp.where(first, head, tail).astype(far_ref.dtype)
 
     @pl.when(lead_ref[0] != 0)
     def _():
@@ -136,9 +139,11 @@
 
 def outer_kernel(
     side_ref, near_ref, rest_ref, far_ref, saved_ref, mid_ref, inner_ref, weight_ref, offset_ref,
-    whole_ref, edge_ref, even, odd,
+    whole_ref, edge_ref, halo, even, odd,
 ):
-    all_views, rows, _, chans = near_ref.shape
+    reach, lines, chans = near_ref.shape
+    all_views = mid_ref.shape[0]
+    rows = lines // all_views
     layers = weight_ref.shape[0]
     bufs = (even, odd)
     groups = even.shape[0]
@@ -147,27 +152,44 @@
     first = side_ref[0] == 0
     place = lax.broadcasted_iota(jnp.int32, (views, TILE, chans), 1)
     whole_ref[:, :mid] = mid_ref[...]
+    for place_at in (0, TILE - 1):
+        halo[pl.ds(place_at, lines, stride=TILE)] = jnp.zeros((lines, chans), jnp.float32)
+    for c in range(reach):
+        near = near_ref[c].astype(jnp.float32) + rest_ref[c].astype(jnp.float32)
+        far = far_ref[c].astype(jnp.float32)
+        halo[pl.ds(EDGE - reach + c, lines, stride=TILE)] = jnp.where(first, far, near)
+        halo[pl.ds(EDGE + c, lines, stride=TILE)] = jnp.where(first, near, far)
 
     def kept(layer, row, group):
         part = saved_ref[layer, row, group * views * TILE : (group + 1) * views * TILE]
         return part.astype(jnp.float32).reshape(views, TILE, chans)
 
+    def put_windows(dst, row, lower, upper, layer):
+        for shift in range(3):
+            window = jnp.where(
+                place < EDGE,
+                pltpu.roll(lower, TILE - 1 - layer - shift, 1),
+                pltpu.roll(upper, EDGE - 1 + layer - shift, 1),
+            )
+            dst[shift, row] = window.reshape(views * TILE, chans).astype(dst.dtype)
+
     for group in range(groups):
         for buf in bufs:
             clear_borders(buf.at[group])
-        span = slice(group * views, (group + 1) * views)
         for row in range(rows):
-            near = near_ref[span, row].astype(jnp.float32) + rest_ref[span, row].astype(jnp.float32)
-            far = far_ref[span, row].astype(jnp.float32)
-            right = jnp.where(first, near, far)
-            left = jnp.where(first, far, near)
             own = kept(0, row, group)
-            cells = jnp.concatenate([left, own[:, EDGE:], own[:, :EDGE], right], axis=1)
-            put_shifted(even.at[group], row + 1, cells)
+            ends = jnp.stack(
+                [
+                    halo[(view * rows + row) * TILE : (view * rows + row + 1) * TILE]
+                    for view in range(group * views, (group + 1) * views)
+                ]
+            )
+            lower = jnp.where(place < EDGE, ends, own)
+            upper = jnp.where(place < EDGE, own, ends)
+            put_windows(even.at[group], row + 1, lower, upper, 0)
     for layer in range(layers):
         weight = spatial_weight(weight_ref, layer)
         offset = offset_ref[layer : layer + 1]
-        fresh = layer + 1
         for group in range(groups):
             src, dst = bufs[layer % 2].at[group], bufs[(layer + 1) % 2].at[group]
             stacked = jnp.concatenate(
@@ -179,32 +201,33 @@
                 axis=1,
             )
             total = jnp.dot(stacked, weight, preferred_element_type=jnp.float32)
-            span = views * 2 * TILE
+            span = views * TILE
             part = slice(group * views, (group + 1) * views)
             for pair in range(rows // 2):
-                ends = []
-                for r in range(2):
-                    value = gelu(
+                values = [
+                    gelu(
                         total[pair * span : (pair + 1) * span, r * chans : (r + 1) * chans] + offset
-                    ).reshape(views, 2 * TILE, chans)
-                    lower, upper = value[:, :TILE], value[:, TILE:]
-                    row = 2 * pair + r
-                    if layer == layers - 1:
-                        ends.append((lower, upper))
-                    else:
-                        own = kept(fresh, row, group)
-                        lower = jnp.where(place >= EDGE + fresh, own, lower)
-                        upper = jnp.where(place < EDGE - fresh, own, upper)
-                        put_shifted(dst, row + 1, jnp.concatenate([lower, upper], axis=1))
-                if ends:
-                    own = inner_ref[part, 2 * TILE * pair : 2 * TILE * (pair + 1)].astype(jnp.float32)
-                    done = []
-                    for r, (lower, upper) in enumerate(ends):
-                        tile = own[:, r * TILE : (r + 1) * TILE]
-                        tile = jnp.where((place >= EDGE) & (place < EDGE + fresh), lower, tile)
-                        done.append(jnp.where((place < EDGE) & (place >= EDGE - fresh), upper, tile))
-                    done = jnp.concatenate(done, axis=1).astype(edge_ref.dtype)
-                    edge_ref[part, 2 * TILE * pair : 2 * TILE * (pair + 1)] = done
+                    ).reshape(views, TILE, chans)
+                    for r in range(2)
+                ]
+                if layer < layers - 1:
+                    for r, value in enumerate(values):
+                        own = kept(layer + 1, 2 * pair + r, group)
+                        lower = jnp.where(place > EDGE + layer, own, pltpu.roll(value, 2 + layer, 1))
+                        upper = jnp.where(place < EDGE - 1 - layer, own, pltpu.roll(value, TILE - 2 - layer, 1))
+                        put_windows(dst, 2 * pair + r + 1, lower, upper, layer + 1)
+                else:
+                    block = slice(2 * TILE * pair, 2 * TILE * (pair + 1))
+                    own = inner_ref[part, block].astype(jnp.float32)
+                    kept_place = (place == 0) | (place == TILE - 1)
+                    done = jnp.concatenate(
+                        [
+                            jnp.where(kept_place, own[:, r * TILE : (r + 1) * TILE], pltpu.roll(value, EDGE, 1))
+                            for r, value in enumerate(values)
+                        ],
+                        axis=1,
+                    ).astype(edge_ref.dtype)
+                    edge_ref[part, block] = done
                     whole_ref[part, mid + 2 * TILE * pair : mid + 2 * TILE * (pair + 1)] = done
 
 
@@ -279,7 +302,7 @@
     views, rows, cols, chans = light_field.shape
     lon_count, view_count = lax.axis_size("lon"), lax.axis_size("view")
     lon, view = lax.axis_index("lon"), lax.axis_index("view")
-    lead = ((lon == 0) & (view > 0) & (view < view_count - 1)).astype(jnp.int32)[None]
+    lead = ((lon == 0) & (view > 0)).astype(jnp.int32)[None]
     lon_side, view_side = lax.rem(lon, 2)[None], lax.rem(view, 2)[None]
     layers = spatial_weights.shape[0]
     half = jnp.bfloat16
@@ -287,7 +310,7 @@
     def shaped(*shape):
         return jax.ShapeDtypeStruct(shape, half)
 
-    edges = shaped(views, rows, EDGE, chans)
+    edges = shaped(layers, views * rows, chans)
     inner_shapes = (
         shaped(views, rows * (cols - TILE), chans),
         shaped(views, rows * TILE, chans),
@@ -303,6 +326,7 @@
         out_specs=(VMEM,) * 7,
         scratch_shapes=[
             pltpu.VMEM((2, views, rows, TILE, chans), half),
+            pltpu.VMEM((2, views * rows * TILE, chans), jnp.float32),
             pltpu.VMEM(light_field.shape, half),
             pltpu.VMEM(spatial_weights.shape, half),
             *inner_scratch,
@@ -336,7 +360,8 @@
         out_shape=(shaped(views, rows * cols, chans), inner_shapes[1]),
         in_specs=[SMEM] + [VMEM] * 8,
         out_specs=(VMEM, VMEM),
-        scratch_shapes=[pltpu.VMEM((GROUPS, 3, rows + 2, views // GROUPS * 2 * TILE, chans), half)] * 2,
+        scratch_shapes=[pltpu.VMEM((views * rows * TILE, chans), jnp.float32)]
+        + [pltpu.VMEM((GROUPS, 3, rows + 2, views // GROUPS * TILE, chans), half)] * 2,
         compiler_params=params(6),
         name="outer",
     )(lon_side, near_lead, near_rest, far, saved, mid, edge, spatial_weights, spatial_bias)

time: 73.2 us -> 72.6 us (level)
  no operation moved by 1% of the time
where the time goes in v5:
time: 72.6 us; the launch traced here: 72.3 us
  starting transfers between devices  54 us (74%)
  Pallas kernels  11.1 us (15%)
  waiting for transfers between devices  7.1 us (10%)
    ppermute x1, starting transfers between devices, local(): lax.ppermute(far, 'lon', neighbours(range(1, lon_count, 2), lon_count, Tr...  41.1 us
    pallas_call x1, Pallas kernels, local(): pl.pallas_call(pack_kernel, out_shape=(edges, edges, *biases, *inner_shap...  5.99 us
    ppermute x1, waiting for transfers between devices, local(): far_edge = lax.ppermute(edge, 'view', far_views)  4.3 us
    ppermute x1, starting transfers between devices, local(): lax.ppermute(whole, 'view', neighbours(range(0, view_count, 2), view_count))  3.96 us
    ppermute x1, starting transfers between devices, local(): mid_lead = lax.ppermute(early[0], ('lon', 'view'), far_views)  3.19 us
    ppermute x1, waiting for transfers between devices, local(): near_lead = lax.ppermute(near, 'lon', neighbours(range(0, 2, 2), lon_count))  2.78 us
    ppermute x1, starting transfers between devices, local(): far_edge = lax.ppermute(edge, 'view', far_views)  2.44 us
    pallas_call x1, Pallas kernels, local(): pl.pallas_call(outer_kernel, out_shape=(shaped(views, rows * cols, chans)...  2.23 us
  transfers between devices with their start and end apart: 7, of which 2 were waited for; matrix products, arithmetic and copies ran while one was open for 0% of the time, Pallas kernels for 2%

profile of v5, /device:TPU:33, one launch (start us, length us, event | category | flops | bytes accessed | tf_op | source)
XLA Modules:
  0.0 72.3 jit_solution(7203185420093446228)
XLA Ops:
  0.0 0.0 copy-start
  0.0 0.0 copy-start.1
  0.0 6.0 %pack.1 = (bf16[3,64,128]{2,1,0:T(8,128)(2,1)S(1)}, bf16[3,64,128]{2,1,0:T(8,128)(2,1)S(1)}, f32[3,128]{1,0:T(4,128)S(1)}, f32[1,128]{1,0:T(1,128)S(1)}, bf16[8,...) custom-call(s32[1]{0:T(128)} %bitcast.1.side_ref, ...), custom_call_target="tpu_custom_call" | custom-call | flops 2000000000 | bytes 10000000 | tf_op jit(solution)/shard_map/pack/pallas_call | solution.py:322
  6.0 41.1 %collective-permute-start.2 = (bf16[3,64,128]{2,1,0:T(8,128)(2,1)S(1)}, bf16[3,64,128]{2,1,0:T(8,128)(2,1)S(1)}, u32[]{:S(2)}, u32[]{:S(2)}) collective-permute-start(bf16[3,64,128]{2,1,0:T(8,128)(2,1)S(1)} %get-tuple-element.18), channel_id=1, source_target_pairs={{8,16},{16,8},{24,32},{32,24},{40,48},{48,40},{56,64},{64,56},{72,... | collective-permute-start | bytes 147464 | tf_op jit(solution)/shard_map/ppermute | solution.py:345
  47.1 0.7 collective-permute-start.1
  47.8 2.0 %collective-permute-start = (bf16[3,64,128]{2,1,0:T(8,128)(2,1)S(1)}, bf16[3,64,128]{2,1,0:T(8,128)(2,1)S(1)}, u32[]{:S(2)}, u32[]{:S(2)}) collective-permute-start(bf16[3,64,128]{2,1,0:T(8,128)(2,1)S(1)} %get-tuple-element.17), channel_id=1, source_target_pairs={{0,8},{8,0},{1,9},{9,1},{2,10},{10,2},{3,11},{11,3},{4,12},{12,4},... | collective-permute-start | bytes 147464 | tf_op jit(solution)/shard_map/ppermute | solution.py:343
  49.7 0.0 copy-done
  49.7 0.0 copy-done.1
  49.7 0.1 inner.1
  49.8 0.0 collective-permute-done.2.far_ref
  49.8 0.0 collective-permute-done.1.rest_ref
  49.8 2.8 %collective-permute-done.near_ref = bf16[3,64,128]{2,1,0:T(8,128)(2,1)S(1)} collective-permute-done((bf16[3,64,128]{2,1,0:T(8,128)(2,1)S(1)}, bf16[3,64,128]{2,1,0:T(8,128)(2,1)S(1)}, u32[]{:S(2)}, u32[]{:S(2)}) %collective-permute-start) | collective-permute-done | bytes 49184 | tf_op jit(solution)/shard_map/ppermute | solution.py:343
  52.6 0.0 copy-start.2
  52.6 2.2 %outer.1 = (bf16[8,256,128]{2,1,0:T(8,128)(2,1)S(1)}, bf16[8,64,128]{2,1,0:T(8,128)(2,1)}) custom-call(s32[1]{0:T(128)} %bitcast.1.side_ref, bf16[3,64,128]{2,1,0:T(8,128)(2,1)S(1)} %collective-permute-done.near_ref, bf16[3,64,128]{2,1,0:T(8,128)(2,1)S(1)} %collective-permute-done.1.rest_ref, bf16[3,64,128]{2,1,0:T(8,128)(2,1)S(1)} %collective-permute-done.2.far_ref, ...), custom_call_target="tpu_custom_call" | custom-call | tf_op jit(solution)/shard_map/outer/pallas_call | solution.py:358
  54.8 4.0 %collective-permute-start.3 = (bf16[8,256,128]{2,1,0:T(8,128)(2,1)S(1)}, bf16[8,256,128]{2,1,0:T(8,128)(2,1)S(1)}, u32[]{:S(2)}, u32[]{:S(2)}) collective-permute-start(bf16[8,256,128]{2,1,0:T(8,128)(2,1)S(1)} %get-tuple-element.26.hidden_ref), channel_id=1, source_target_pairs={{0,1},{1,0},{2,3},{3,2},{4,5},{5,4},{6,7},{7,6},{8,9},{9,8},{10,11... | collective-permute-start | bytes 1572872 | tf_op jit(solution)/shard_map/ppermute | solution.py:369
  58.8 3.2 %collective-permute-start.4 = (bf16[8,192,128]{2,1,0:T(8,128)(2,1)S(1)}, bf16[8,192,128]{2,1,0:T(8,128)(2,1)S(1)}, u32[]{:S(2)}, u32[]{:S(2)}) collective-permute-start(bf16[8,192,128]{2,1,0:T(8,128)(2,1)S(1)} %get-tuple-element.20.mid_in), channel_id=1, source_target_pairs={{1,2},{2,1},{3,4},{4,3},{5,6},{6,5},{257,258},{258,257},{259,260},... | collective-permute-start | bytes 1179656 | tf_op jit(solution)/shard_map/ppermute | solution.py:344
  62.0 0.7 collective-permute-start.5
  62.7 2.4 %collective-permute-start.6 = (bf16[8,64,128]{2,1,0:T(8,128)(2,1)}, bf16[8,64,128]{2,1,0:T(8,128)(2,1)}, u32[]{:S(2)}, u32[]{:S(2)}) collective-permute-start(bf16[8,64,128]{2,1,0:T(8,128)(2,1)} %get-tuple-element.27), channel_id=1, source_target_pairs={{1,2},{2,1},{3,4},{4,3},{5,6},{6,5},{9,10},{10,9},{11,12},{12,11},... | collective-permute-start | bytes 393224 | tf_op jit(solution)/shard_map/ppermute | solution.py:368
  65.2 4.3 %collective-permute-done.6.edge_ref = bf16[8,64,128]{2,1,0:T(8,128)(2,1)} collective-permute-done((bf16[8,64,128]{2,1,0:T(8,128)(2,1)}, bf16[8,64,128]{2,1,0:T(8,128)(2,1)}, u32[]{:S(2)}, u32[]{:S(2)}) %collective-permute-start.6) | collective-permute-done | bytes 131104 | tf_op jit(solution)/shard_map/ppermute | solution.py:368
  69.5 0.0 collective-permute-done.4.lead_ref
  69.5 0.0 collective-permute-done.5.rest_ref
  69.5 0.0 copy-done.2
  69.5 1.5 %partial.1.partial_ref = f32[4,256,256]{2,1,0:T(8,128)S(1)} custom-call(s32[1]{0:T(128)} %bitcast.side_ref, bf16[8,256,128]{2,1,0:T(8,128)(2,1)S(1)} %get-tuple-element.26.hidden_ref, bf16[8,192,128]{2,1,0:T(8,128)(2,1)S(1)} %collective-permute-done.4.lead_ref, bf16[8,192,128]{2,1,0:T(8,128)(2,1)S(1)} %collective-permute-done.5.rest_ref, ...), custom_call_target="tpu_custom_call" | custom-call | tf_op jit(solution)/shard_map/partial/pallas_call | solution.py:370
  71.0 0.0 collective-permute-done.3.near_ref
  71.0 1.3 %final.1 = bf16[8,8,32,128]{3,2,1,0:T(8,128)(2,1)} custom-call(s32[1]{0:T(128)} %bitcast.side_ref, bf16[8,256,128]{2,1,0:T(8,128)(2,1)S(1)} %collective-permute-done.3.near_ref, f32[4,256,256]{2,1,0:T(8,128)S(1)} %partial.1.partial_ref, bf16[3,3,128,128]{3,2,1,0:T(8,128)(2,1)S(1)} %copy-done.2, bf16[8,8,32,128]{3,2,1,0:T(8,128)(2,1)S(1)} %copy-done.1), custom_call_target="tpu_custom_call" | custom-call | tf_op jit(solution)/shard_map/final/pallas_call | solution.py:378
Async XLA Ops:
  0.0 49.7 %copy-start = (bf16[3,3,3,128,128]{4,3,2,1,0:T(8,128)(2,1)S(1)}, bf16[3,3,3,128,128]{4,3,2,1,0:T(8,128)(2,1)}, u32[]{:S(2)}) copy-start(bf16[3,3,3,128,128]{4,3,2,1,0:T(8,128)(2,1)} %weight_ref.5) | copy-start | bytes 2654212
  0.0 49.7 %copy-start.1 = (bf16[8,8,32,128]{3,2,1,0:T(8,128)(2,1)S(1)}, bf16[8,8,32,128]{3,2,1,0:T(8,128)(2,1)}, u32[]{:S(2)}) copy-start(bf16[8,8,32,128]{3,2,1,0:T(8,128)(2,1)} %field_ref.3) | copy-start | bytes 1572868
  6.0 43.8 %collective-permute-start.2 = (bf16[3,64,128]{2,1,0:T(8,128)(2,1)S(1)}, bf16[3,64,128]{2,1,0:T(8,128)(2,1)S(1)}, u32[]{:S(2)}, u32[]{:S(2)}) collective-permute-start(bf16[3,64,128]{2,1,0:T(8,128)(2,1)S(1)} %get-tuple-element.18), channel_id=1, source_target_pairs={{8,16},{16,8},{24,32},{32,24},{40,48},{48,40},{56,64},{64,56},{72,... | collective-permute-start | bytes 147464 | tf_op jit(solution)/shard_map/ppermute | solution.py:345
  47.1 2.7 %collective-permute-start.1 = (bf16[3,64,128]{2,1,0:T(8,128)(2,1)S(1)}, bf16[3,64,128]{2,1,0:T(8,128)(2,1)S(1)}, u32[]{:S(2)}, u32[]{:S(2)}) collective-permute-start(bf16[3,64,128]{2,1,0:T(8,128)(2,1)S(1)} %get-tuple-element.17), channel_id=1, source_target_pairs={{16,24},{24,16},{32,40},{40,32},{48,56},{56,48},{64,72},{72,64},{8... | collective-permute-start | bytes 147464 | tf_op jit(solution)/shard_map/ppermute | solution.py:346
  47.8 4.9 %collective-permute-start = (bf16[3,64,128]{2,1,0:T(8,128)(2,1)S(1)}, bf16[3,64,128]{2,1,0:T(8,128)(2,1)S(1)}, u32[]{:S(2)}, u32[]{:S(2)}) collective-permute-start(bf16[3,64,128]{2,1,0:T(8,128)(2,1)S(1)} %get-tuple-element.17), channel_id=1, source_target_pairs={{0,8},{8,0},{1,9},{9,1},{2,10},{10,2},{3,11},{11,3},{4,12},{12,4},... | collective-permute-start | bytes 147464 | tf_op jit(solution)/shard_map/ppermute | solution.py:343
  52.6 16.8 %copy-start.2 = (bf16[3,3,128,128]{3,2,1,0:T(8,128)(2,1)S(1)}, bf16[3,3,128,128]{3,2,1,0:T(8,128)(2,1)}, u32[]{:S(2)}) copy-start(bf16[3,3,128,128]{3,2,1,0:T(8,128)(2,1)} %weight_ref.7) | copy-start | bytes 884740
  54.8 16.2 %collective-permute-start.3 = (bf16[8,256,128]{2,1,0:T(8,128)(2,1)S(1)}, bf16[8,256,128]{2,1,0:T(8,128)(2,1)S(1)}, u32[]{:S(2)}, u32[]{:S(2)}) collective-permute-start(bf16[8,256,128]{2,1,0:T(8,128)(2,1)S(1)} %get-tuple-element.26.hidden_ref), channel_id=1, source_target_pairs={{0,1},{1,0},{2,3},{3,2},{4,5},{5,4},{6,7},{7,6},{8,9},{9,8},{10,11... | collective-permute-start | bytes 1572872 | tf_op jit(solution)/shard_map/ppermute | solution.py:369
  58.8 10.6 %collective-permute-start.4 = (bf16[8,192,128]{2,1,0:T(8,128)(2,1)S(1)}, bf16[8,192,128]{2,1,0:T(8,128)(2,1)S(1)}, u32[]{:S(2)}, u32[]{:S(2)}) collective-permute-start(bf16[8,192,128]{2,1,0:T(8,128)(2,1)S(1)} %get-tuple-element.20.mid_in), channel_id=1, source_target_pairs={{1,2},{2,1},{3,4},{4,3},{5,6},{6,5},{257,258},{258,257},{259,260},... | collective-permute-start | bytes 1179656 | tf_op jit(solution)/shard_map/ppermute | solution.py:344
  62.0 7.4 %collective-permute-start.5 = (bf16[8,192,128]{2,1,0:T(8,128)(2,1)S(1)}, bf16[8,192,128]{2,1,0:T(8,128)(2,1)S(1)}, u32[]{:S(2)}, u32[]{:S(2)}) collective-permute-start(bf16[8,192,128]{2,1,0:T(8,128)(2,1)S(1)} %get-tuple-element.24.mid_ref), channel_id=1, source_target_pairs={{9,10},{10,9},{11,12},{12,11},{13,14},{14,13},{17,18},{18,17},{19,... | collective-permute-start | bytes 1179656 | tf_op jit(solution)/shard_map/ppermute | solution.py:357
  62.7 6.7 %collective-permute-start.6 = (bf16[8,64,128]{2,1,0:T(8,128)(2,1)}, bf16[8,64,128]{2,1,0:T(8,128)(2,1)}, u32[]{:S(2)}, u32[]{:S(2)}) collective-permute-start(bf16[8,64,128]{2,1,0:T(8,128)(2,1)} %get-tuple-element.27), channel_id=1, source_target_pairs={{1,2},{2,1},{3,4},{4,3},{5,6},{6,5},{9,10},{10,9},{11,12},{12,11},... | collective-permute-start | bytes 393224 | tf_op jit(solution)/shard_map/ppermute | solution.py:368

commit v6 on v5

--- a/solution.py
+++ b/solution.py
@@ -9,6 +9,8 @@
 EDGE = 4
 TILE = 8
 GROUPS = 2
+LEAD = 2
+LEAD_GROUPS = 1
 VMEM = pl.BlockSpec(memory_space=pltpu.VMEM)
 SMEM = pl.BlockSpec(memory_space=pltpu.SMEM)
 HBM = pl.BlockSpec(memory_space=pl.ANY)
@@ -47,33 +49,41 @@
             buf[shift, row] = jnp.zeros(buf.shape[2:], buf.dtype)
 
 
-def pack_kernel(
-    side_ref, lead_ref, field_hbm, weight_hbm, spatial_hbm, angular_hbm,
-    near_ref, far_ref, spatial_ref, angular_ref, mid_ref, edge_ref, saved_ref,
-    tiles, columns, field, weight, even, odd, sems,
-):
-    cols = field_hbm.shape[2]
-    reach, lines, chans = near_ref.shape
-    copies = [
-        pltpu.make_async_copy(field_hbm.at[:, :, pl.ds(start, TILE)], tiles.at[i], sems.at[i])
-        for i, start in enumerate((0, cols - TILE))
-    ]
-    copies.append(pltpu.make_async_copy(spatial_hbm, spatial_ref, sems.at[2]))
-    copies.append(pltpu.make_async_copy(angular_hbm, angular_ref, sems.at[3]))
-    for copy in copies:
-        copy.start()
-    for copy in copies:
-        copy.wait()
+def take_edges(side_ref, columns, near_ref, far_ref):
+    reach, lines, _ = near_ref.shape
     first = side_ref[0] == 0
-    for i in range(2):
-        columns[i] = tiles[i].astype(jnp.float32).reshape(lines * TILE, chans)
     for c in range(reach):
         head = columns[0, pl.ds(c, lines, stride=TILE)]
         tail = columns[1, pl.ds(TILE - reach + c, lines, stride=TILE)]
         near_ref[c] = jnp.where(first, tail, head).astype(near_ref.dtype)
-        far_ref[c] = jnp.where(first, head, tail).astype(far_ref.dtype)
-
-    @pl.when(lead_ref[0] != 0)
+        if far_ref is not None:
+            far_ref[c] = jnp.where(first, head, tail).astype(far_ref.dtype)
+
+
+def early_kernel(
+    side_ref, lead_ref, field_hbm, weight_hbm, spatial_hbm, angular_hbm,
+    near_ref, spatial_ref, angular_ref, mid_ref, edge_ref, saved_ref,
+    tiles, columns, field, weight, even, odd, sems,
+):
+    cols = field_hbm.shape[2]
+
+    @pl.when(lead_ref[0] > 0)
+    def _():
+        copies = [
+            pltpu.make_async_copy(field_hbm.at[:, :, pl.ds(start, TILE)], tiles.at[i], sems.at[i])
+            for i, start in enumerate((0, cols - TILE))
+        ]
+        copies.append(pltpu.make_async_copy(spatial_hbm, spatial_ref, sems.at[2]))
+        copies.append(pltpu.make_async_copy(angular_hbm, angular_ref, sems.at[3]))
+        for copy in copies:
+            copy.start()
+        for copy in copies:
+            copy.wait()
+        for i in range(2):
+            columns[i] = tiles[i].astype(jnp.float32).reshape(columns.shape[1:])
+        take_edges(side_ref, columns, near_ref, None)
+
+    @pl.when(lead_ref[0] == LEAD)
     def _():
         loads = (
             pltpu.make_async_copy(field_hbm, field, sems.at[0]),
@@ -86,19 +96,54 @@
         inner_layers(field, weight, spatial_ref, mid_ref, edge_ref, saved_ref, even, odd)
 
 
+def edges_kernel(
+    side_ref, lead_ref, field_ref, spatial_ref, first_ref, saved_ref, inner_ref, weight_hbm,
+    near_ref, far_ref, edge_ref,
+    columns, weight, halo, even, odd, sem,
+):
+    cols = field_ref.shape[2]
+    for i, start in enumerate((0, cols - TILE)):
+        columns[i] = field_ref[:, :, start : start + TILE].astype(jnp.float32).reshape(columns.shape[1:])
+    take_edges(side_ref, columns, near_ref, far_ref)
+
+    @pl.when(lead_ref[0] == LEAD)
+    def _():
+        load = pltpu.make_async_copy(weight_hbm, weight, sem)
+        load.start()
+        load.wait()
+        put_halo(halo, first_ref, None, None, None)
+        outer_layers("rr", halo, saved_ref, inner_ref, weight, spatial_ref, ((edge_ref, 0),), even, odd, 1)
+
+
 def inner_kernel(
-    lead_ref, field_ref, weight_ref, offset_ref, mid_in, edge_in, saved_in,
-    mid_ref, edge_ref, saved_ref, even, odd,
+    lead_ref, field_ref, weight_ref, spatial_in, angular_in, mid_in, edge_in, saved_in, spatial_hbm, angular_hbm,
+    mid_ref, edge_ref, saved_ref, spatial_ref, angular_ref, even, odd, sems,
 ):
-    @pl.when(lead_ref[0] != 0)
+    @pl.when(lead_ref[0] > 0)
+    def _():
+        spatial_ref[...] = spatial_in[...]
+        angular_ref[...] = angular_in[...]
+
+    @pl.when(lead_ref[0] == 0)
+    def _():
+        copies = (
+            pltpu.make_async_copy(spatial_hbm, spatial_ref, sems.at[0]),
+            pltpu.make_async_copy(angular_hbm, angular_ref, sems.at[1]),
+        )
+        for copy in copies:
+            copy.start()
+        for copy in copies:
+            copy.wait()
+
+    @pl.when(lead_ref[0] == LEAD)
     def _():
         mid_ref[...] = mid_in[...]
         edge_ref[...] = edge_in[...]
         saved_ref[...] = saved_in[...]
 
-    @pl.when(lead_ref[0] == 0)
-    def _():
-        inner_layers(field_ref, weight_ref, offset_ref, mid_ref, edge_ref, saved_ref, even, odd)
+    @pl.when(lead_ref[0] != LEAD)
+    def _():
+        inner_layers(field_ref, weight_ref, spatial_ref, mid_ref, edge_ref, saved_ref, even, odd)
 
 
 def inner_layers(field_ref, weight_ref, offset_ref, mid_ref, edge_ref, saved_ref, even, odd):
@@ -137,56 +182,67 @@
                     keep(layer + 1, 2 * pair + r, cells[r])
 
 
-def outer_kernel(
-    side_ref, near_ref, rest_ref, far_ref, saved_ref, mid_ref, inner_ref, weight_ref, offset_ref,
-    whole_ref, edge_ref, halo, even, odd,
-):
-    reach, lines, chans = near_ref.shape
-    all_views = mid_ref.shape[0]
-    rows = lines // all_views
-    layers = weight_ref.shape[0]
-    bufs = (even, odd)
-    groups = even.shape[0]
-    views = all_views // groups
-    mid = mid_ref.shape[1]
-    first = side_ref[0] == 0
-    place = lax.broadcasted_iota(jnp.int32, (views, TILE, chans), 1)
-    whole_ref[:, :mid] = mid_ref[...]
-    for place_at in (0, TILE - 1):
-        halo[pl.ds(place_at, lines, stride=TILE)] = jnp.zeros((lines, chans), jnp.float32)
+def put_halo(halo, near_ref, rest_ref, far_ref, first):
+    reach, lines, _ = near_ref.shape
+    halo[...] = jnp.zeros(halo.shape, halo.dtype)
     for c in range(reach):
-        near = near_ref[c].astype(jnp.float32) + rest_ref[c].astype(jnp.float32)
+        near = near_ref[c].astype(jnp.float32)
+        if rest_ref is None:
+            halo[pl.ds(EDGE + c, lines, stride=TILE)] = near
+            continue
+        near = near + rest_ref[c].astype(jnp.float32)
         far = far_ref[c].astype(jnp.float32)
         halo[pl.ds(EDGE - reach + c, lines, stride=TILE)] = jnp.where(first, far, near)
         halo[pl.ds(EDGE + c, lines, stride=TILE)] = jnp.where(first, near, far)
 
+
+def outer_layers(mode, halo, saved_ref, inner_ref, weight_ref, offset_ref, edge_refs, even, odd, groups):
+    layers, rows = saved_ref.shape[:2]
+    chans = weight_ref.shape[-1]
+    all_views = inner_ref.shape[0]
+    views = all_views // groups
+    tiles = views if mode == "lr" else views // 2
+    width = tiles * TILE
+    place = lax.broadcasted_iota(jnp.int32, (tiles, TILE, chans), 1)
+    bufs = (even, odd)
+
+    def halves(cells):
+        if mode == "lr":
+            return cells, cells
+        cells = cells.reshape(tiles, 2, TILE, chans)
+        return cells[:, 0], cells[:, 1]
+
+    def roll(cells, amount):
+        return pltpu.roll(cells, amount % TILE, 1) if amount % TILE else cells
+
     def kept(layer, row, group):
         part = saved_ref[layer, row, group * views * TILE : (group + 1) * views * TILE]
-        return part.astype(jnp.float32).reshape(views, TILE, chans)
-
-    def put_windows(dst, row, lower, upper, layer):
+        return halves(part.astype(jnp.float32).reshape(views, TILE, chans))
+
+    def put_windows(dst, row, bases, layer):
         for shift in range(3):
-            window = jnp.where(
-                place < EDGE,
-                pltpu.roll(lower, TILE - 1 - layer - shift, 1),
-                pltpu.roll(upper, EDGE - 1 + layer - shift, 1),
-            )
-            dst[shift, row] = window.reshape(views * TILE, chans).astype(dst.dtype)
+            taken = [
+                roll(base, EDGE * half - (1 + layer + shift if kind == "l" else 1 - layer + shift))
+                for half, (kind, base) in enumerate(zip(mode, bases))
+            ]
+            window = jnp.where(place < EDGE, taken[0], taken[1])
+            dst[shift, row, :width] = window.reshape(width, chans).astype(dst.dtype)
 
     for group in range(groups):
         for buf in bufs:
             clear_borders(buf.at[group])
         for row in range(rows):
-            own = kept(0, row, group)
             ends = jnp.stack(
                 [
                     halo[(view * rows + row) * TILE : (view * rows + row + 1) * TILE]
                     for view in range(group * views, (group + 1) * views)
                 ]
             )
-            lower = jnp.where(place < EDGE, ends, own)
-            upper = jnp.where(place < EDGE, own, ends)
-            put_windows(even.at[group], row + 1, lower, upper, 0)
+            bases = [
+                jnp.where((place < EDGE) == (kind == "l"), end, own)
+                for kind, end, own in zip(mode, halves(ends), kept(0, row, group))
+            ]
+            put_windows(even.at[group], row + 1, bases, 0)
     for layer in range(layers):
         weight = spatial_weight(weight_ref, layer)
         offset = offset_ref[layer : layer + 1]
@@ -194,41 +250,64 @@
             src, dst = bufs[layer % 2].at[group], bufs[(layer + 1) % 2].at[group]
             stacked = jnp.concatenate(
                 [
-                    jnp.concatenate([src[b, 2 * pair + k] for pair in range(rows // 2)], axis=0)
+                    jnp.concatenate([src[b, 2 * pair + k, :width] for pair in range(rows // 2)], axis=0)
                     for k in range(4)
                     for b in range(3)
                 ],
                 axis=1,
             )
             total = jnp.dot(stacked, weight, preferred_element_type=jnp.float32)
-            span = views * TILE
-            part = slice(group * views, (group + 1) * views)
             for pair in range(rows // 2):
                 values = [
                     gelu(
-                        total[pair * span : (pair + 1) * span, r * chans : (r + 1) * chans] + offset
-                    ).reshape(views, TILE, chans)
+                        total[pair * width : (pair + 1) * width, r * chans : (r + 1) * chans] + offset
+                    ).reshape(tiles, TILE, chans)
                     for r in range(2)
                 ]
                 if layer < layers - 1:
                     for r, value in enumerate(values):
-                        own = kept(layer + 1, 2 * pair + r, group)
-                        lower = jnp.where(place > EDGE + layer, own, pltpu.roll(value, 2 + layer, 1))
-                        upper = jnp.where(place < EDGE - 1 - layer, own, pltpu.roll(value, TILE - 2 - layer, 1))
-                        put_windows(dst, 2 * pair + r + 1, lower, upper, layer + 1)
-                else:
-                    block = slice(2 * TILE * pair, 2 * TILE * (pair + 1))
-                    own = inner_ref[part, block].astype(jnp.float32)
-                    kept_place = (place == 0) | (place == TILE - 1)
-                    done = jnp.concatenate(
-                        [
-                            jnp.where(kept_place, own[:, r * TILE : (r + 1) * TILE], pltpu.roll(value, EDGE, 1))
-                            for r, value in enumerate(values)
-                        ],
-                        axis=1,
-                    ).astype(edge_ref.dtype)
-                    edge_ref[part, block] = done
-                    whole_ref[part, mid + 2 * TILE * pair : mid + 2 * TILE * (pair + 1)] = done
+                        bases = []
+                        for half, (kind, own) in enumerate(zip(mode, kept(layer + 1, 2 * pair + r, group))):
+                            if kind == "l":
+                                fresh, keep = roll(value, 2 + layer - EDGE * half), place > EDGE + layer
+                            else:
+                                fresh, keep = roll(value, 2 - layer - EDGE * half), place < EDGE - 1 - layer
+                            bases.append(jnp.where(keep, own, fresh))
+                        put_windows(dst, 2 * pair + r + 1, bases, layer + 1)
+                    continue
+                part = slice(group * views, (group + 1) * views)
+                block = inner_ref[part, 2 * TILE * pair : 2 * TILE * (pair + 1)].astype(jnp.float32)
+                done = []
+                for r, value in enumerate(values):
+                    outs = list(halves(block[:, r * TILE : (r + 1) * TILE]))
+                    for half, kind in enumerate(mode):
+                        if kind == "l":
+                            fresh, new = roll(value, EDGE - EDGE * half), (place >= EDGE) & (place < TILE - 1)
+                        else:
+                            fresh, new = roll(value, -EDGE * half), (place < EDGE) & (place > 0)
+                        at = 0 if mode == "lr" else half
+                        outs[at] = jnp.where(new, fresh, outs[at])
+                    done.append(outs[0] if mode == "lr" else jnp.stack(outs, axis=1).reshape(views, TILE, chans))
+                done = jnp.concatenate(done, axis=1)
+                for ref, start in edge_refs:
+                    ref[part, start + 2 * TILE * pair : start + 2 * TILE * (pair + 1)] = done.astype(ref.dtype)
+
+
+def outer_kernel(
+    side_ref, lead_ref, near_ref, rest_ref, far_ref, saved_ref, mid_ref, inner_ref, weight_ref, offset_ref,
+    whole_ref, edge_ref, halo, even, odd,
+):
+    mid = mid_ref.shape[1]
+    whole_ref[:, :mid] = mid_ref[...]
+    put_halo(halo, near_ref, rest_ref, far_ref, side_ref[0] == 0)
+    results = ((edge_ref, 0), (whole_ref, mid))
+    for mode, when, groups in (("ll", lead_ref[0] == LEAD, LEAD_GROUPS), ("lr", lead_ref[0] != LEAD, GROUPS)):
+
+        @pl.when(when)
+        def _():
+            outer_layers(
+                mode, halo, saved_ref, inner_ref, weight_ref, offset_ref, results, even, odd, groups
+            )
 
 
 def view_pair(sources, pair, views, blank):
@@ -302,7 +381,7 @@
     views, rows, cols, chans = light_field.shape
     lon_count, view_count = lax.axis_size("lon"), lax.axis_size("view")
     lon, view = lax.axis_index("lon"), lax.axis_index("view")
-    lead = ((lon == 0) & (view > 0)).astype(jnp.int32)[None]
+    lead = ((lon <= 1).astype(jnp.int32) + ((lon == 0) & (view > 0)).astype(jnp.int32))[None]
     lon_side, view_side = lax.rem(lon, 2)[None], lax.rem(view, 2)[None]
     layers = spatial_weights.shape[0]
     half = jnp.bfloat16
@@ -319,14 +398,16 @@
     biases = [jax.ShapeDtypeStruct(b.shape, jnp.float32) for b in (spatial_offsets, angular_offset[None])]
     inner_scratch = [pltpu.VMEM((3, rows + 2, views * cols, chans), half)] * 2
     in_hbm = lambda array: pltpu.with_memory_space_constraint(array, pltpu.HBM)
-    near, far, spatial_bias, angular_bias, *early = pl.pallas_call(
-        pack_kernel,
-        out_shape=(edges, edges, *biases, *inner_shapes),
-        in_specs=[SMEM, SMEM, HBM, HBM, HBM, HBM],
-        out_specs=(VMEM,) * 7,
+    columns = pltpu.VMEM((2, views * rows * TILE, chans), jnp.float32)
+    offsets = in_hbm(spatial_offsets), in_hbm(angular_offset[None])
+    near_first, spatial_first, angular_first, early_mid, early_edge, early_saved = pl.pallas_call(
+        early_kernel,
+        out_shape=(edges, *biases, *inner_shapes),
+        in_specs=[SMEM, SMEM] + [HBM] * 4,
+        out_specs=(VMEM,) * 6,
         scratch_shapes=[
             pltpu.VMEM((2, views, rows, TILE, chans), half),
-            pltpu.VMEM((2, views * rows * TILE, chans), jnp.float32),
+            columns,
             pltpu.VMEM(light_field.shape, half),
             pltpu.VMEM(spatial_weights.shape, half),
             *inner_scratch,
@@ -334,37 +415,56 @@
         ],
         compiler_params=params(12),
         cost_estimate=pl.CostEstimate(flops=2 * 10**9, bytes_accessed=10**7, transcendentals=0),
-        name="pack",
-    )(lon_side, lead, in_hbm(light_field), in_hbm(spatial_weights), in_hbm(spatial_offsets), in_hbm(angular_offset[None]))
+        name="early",
+    )(lon_side, lead, in_hbm(light_field), in_hbm(spatial_weights), *offsets)
     far_views = neighbours(range(1, view_count, 2), view_count)
     rest_views = [
         (line * view_count + i, line * view_count + j) for line in range(1, lon_count) for i, j in far_views
     ]
-    near_lead = lax.ppermute(near, "lon", neighbours(range(0, 2, 2), lon_count))
-    mid_lead = lax.ppermute(early[0], ("lon", "view"), far_views)
+    near_lead = lax.ppermute(near_first, "lon", neighbours(range(0, 2, 2), lon_count))
+    mid_lead = lax.ppermute(early_mid, ("lon", "view"), far_views)
+    near, far, early_edge = pl.pallas_call(
+        edges_kernel,
+        out_shape=(edges, edges, inner_shapes[1]),
+        in_specs=[SMEM, SMEM] + [VMEM] * 5 + [HBM],
+        out_specs=(VMEM,) * 3,
+        scratch_shapes=[
+            columns,
+            pltpu.VMEM(spatial_weights.shape, half),
+            pltpu.VMEM((views * rows * TILE, chans), jnp.float32),
+            *[pltpu.VMEM((1, 3, rows + 2, views * TILE // 2, chans), half)] * 2,
+            pltpu.SemaphoreType.DMA,
+        ],
+        compiler_params=params(8),
+        name="edges",
+    )(
+        lon_side, lead, light_field, spatial_first, near_lead, early_saved, early_edge, in_hbm(spatial_weights)
+    )
     far = lax.ppermute(far, "lon", neighbours(range(1, lon_count, 2), lon_count, True))
     near_rest = lax.ppermute(near, "lon", neighbours(range(2, lon_count, 2), lon_count))
 
-    mid, edge, saved = pl.pallas_call(
+    mid, edge, saved, spatial_bias, angular_bias = pl.pallas_call(
         inner_kernel,
-        out_shape=inner_shapes,
-        in_specs=[SMEM] + [VMEM] * 6,
-        out_specs=(VMEM,) * 3,
-        scratch_shapes=inner_scratch,
+        out_shape=(*inner_shapes, *biases),
+        in_specs=[SMEM] + [VMEM] * 7 + [HBM] * 2,
+        out_specs=(VMEM,) * 5,
+        scratch_shapes=[*inner_scratch, pltpu.SemaphoreType.DMA((2,))],
         compiler_params=params(12),
         name="inner",
-    )(lead, light_field, spatial_weights, spatial_bias, *early)
+    )(
+        lead, light_field, spatial_weights, spatial_first, angular_first, early_mid, early_edge, early_saved, *offsets
+    )
     mid_rest = lax.ppermute(mid, ("lon", "view"), rest_views)
     whole, edge = pl.pallas_call(
         outer_kernel,
         out_shape=(shaped(views, rows * cols, chans), inner_shapes[1]),
-        in_specs=[SMEM] + [VMEM] * 8,
+        in_specs=[SMEM, SMEM] + [VMEM] * 8,
         out_specs=(VMEM, VMEM),
         scratch_shapes=[pltpu.VMEM((views * rows * TILE, chans), jnp.float32)]
         + [pltpu.VMEM((GROUPS, 3, rows + 2, views // GROUPS * TILE, chans), half)] * 2,
         compiler_params=params(6),
         name="outer",
-    )(lon_side, near_lead, near_rest, far, saved, mid, edge, spatial_weights, spatial_bias)
+    )(lon_side, lead, near_lead, near_rest, far, saved, mid, edge, spatial_weights, spatial_bias)
     far_edge = lax.ppermute(edge, "view", far_views)
     near_rows = lax.ppermute(whole, "view", neighbours(range(0, view_count, 2), view_count))
     partial = pl.pallas_call(

time: 72.6 us -> 74.7 us (1.029)
  Pallas kernels: 11.1 us -> 13 us
  waiting for transfers between devices: 7.1 us -> 8.55 us
  starting transfers between devices: 54 us -> 52.7 us
    ppermute x1, starting transfers between devices: 41.1 us -> 35.2 us  [local(): lax.ppermute(far, 'lon', neighbours(range(1, lon_count, 2), lon_count, Tr...]
    ppermute x1, starting transfers between devices: 3.96 us -> 8.54 us  [local(): lax.ppermute(whole, 'view', neighbours(range(0, view_count, 2), view_count))]
    pallas_call x2 -> x3, Pallas kernels: 6.06 us -> 8.42 us  [the longest x1 5.93 us: local(): pl.pallas_call(early_kernel, out_shape=(edges, *biases, *inner_shapes), i...]
    ppermute x1, waiting for transfers between devices: 0.01 us -> 1.33 us  [local(): lax.ppermute(far, 'lon', neighbours(range(1, lon_count, 2), lon_count, Tr...]
    ppermute x2, starting transfers between devices: 5.14 us -> 3.9 us  [the longest x1 1.95 us: local(): lax.ppermute(near_first, 'lon', neighbours(range(0, 2, 2), lon_count))]
    ppermute x1, starting transfers between devices: 2.44 us -> 3.67 us  [local(): far_edge = lax.ppermute(edge, 'view', far_views)]
  transfers between devices with their start and end apart: 7 -> 7, of which waited for: 2 -> 3; matrix products, arithmetic and copies ran while one was open for 0% -> 0% of each run, Pallas kernels for 2% -> 2%
where the time goes in v6:
time: 74.7 us; the launch traced here: 74.4 us
  starting transfers between devices  52.7 us (71%)
  Pallas kernels  13 us (17%)
  waiting for transfers between devices  8.55 us (11%)
    ppermute x1, starting transfers between devices, local(): lax.ppermute(far, 'lon', neighbours(range(1, lon_count, 2), lon_count, Tr...  35.2 us
    ppermute x1, starting transfers between devices, local(): lax.ppermute(whole, 'view', neighbours(range(0, view_count, 2), view_count))  8.54 us
    pallas_call x1, Pallas kernels, local(): pl.pallas_call(early_kernel, out_shape=(edges, *biases, *inner_shapes), i...  5.93 us
    ppermute x1, waiting for transfers between devices, local(): far_edge = lax.ppermute(edge, 'view', far_views)  4.3 us
    ppermute x1, starting transfers between devices, local(): far_edge = lax.ppermute(edge, 'view', far_views)  3.67 us
    ppermute x1, waiting for transfers between devices, local(): lax.ppermute(near_first, 'lon', neighbours(range(0, 2, 2), lon_count))  2.91 us
    pallas_call x1, Pallas kernels, local(): pl.pallas_call(edges_kernel, out_shape=(edges, edges, inner_shapes[1]), i...  2.38 us
    ppermute x1, starting transfers between devices, local(): lax.ppermute(near_first, 'lon', neighbours(range(0, 2, 2), lon_count))  1.95 us
  transfers between devices with their start and end apart: 7, of which 3 were waited for; matrix products, arithmetic and copies ran while one was open for 0% of the time, Pallas kernels for 2%

profile of v6, /device:TPU:33, one launch (start us, length us, event | category | flops | bytes accessed | tf_op | source)
XLA Modules:
  0.0 74.4 jit_solution(1335308120468742156)
XLA Ops:
  0.0 0.0 copy-start.1
  0.0 5.9 %early.1 = (bf16[3,64,128]{2,1,0:T(8,128)(2,1)S(1)}, f32[3,128]{1,0:T(4,128)S(1)}, f32[1,128]{1,0:T(1,128)S(1)}, bf16[8,192,128]{2,1,0:T(8,128)(2,1)S(1)}, bf16[...) custom-call(s32[1]{0:T(128)} %bitcast.1.side_ref, s32[1]{0:T(128)} %bitcast.2.lead_ref, ...), custom_call_target="tpu_custom_call" | custom-call | flops 2000000000 | bytes 10000000 | tf_op jit(solution)/shard_map/early/pallas_call | solution.py:403
  5.9 2.0 %collective-permute-start = (bf16[3,64,128]{2,1,0:T(8,128)(2,1)S(1)}, bf16[3,64,128]{2,1,0:T(8,128)(2,1)S(1)}, u32[]{:S(2)}, u32[]{:S(2)}) collective-permute-start(bf16[3,64,128]{2,1,0:T(8,128)(2,1)S(1)} %get-tuple-element.21), channel_id=1, source_target_pairs={{0,8},{8,0},{1,9},{9,1},{2,10},{10,2},{3,11},{11,3},{4,12},{12,4},... | collective-permute-start | bytes 147464 | tf_op jit(solution)/shard_map/ppermute | solution.py:424
  7.9 2.9 %collective-permute-done.first_ref.near_ref = bf16[3,64,128]{2,1,0:T(8,128)(2,1)S(1)} collective-permute-done((bf16[3,64,128]{2,1,0:T(8,128)(2,1)S(1)}, bf16[3,64,128]{2,1,0:T(8,128)(2,1)S(1)}, u32[]{:S(2)}, u32[]{:S(2)}) %collective-permute-start) | collective-permute-done | bytes 49184 | tf_op jit(solution)/shard_map/ppermute | solution.py:424
  10.8 0.0 copy-done.1
  10.8 0.0 copy-start
  10.8 2.4 %edges.1 = (bf16[3,64,128]{2,1,0:T(8,128)(2,1)S(1)}, bf16[3,64,128]{2,1,0:T(8,128)(2,1)S(1)}, bf16[8,64,128]{2,1,0:T(8,128)(2,1)S(1)}) custom-call(s32[1]{0:T(128)} %bitcast.1.side_ref, s32[1]{0:T(128)} %bitcast.2.lead_ref, bf16[8,8,32,128]{3,2,1,0:T(8,128)(2,1)S(1)} %copy-done.1, f32[3,128]{1,0:T(4,128)S(1)} %get-tuple-element.22.spatial_ref.spatial_in, ...), custom_call_target="tpu_custom_call" | custom-call | tf_op jit(solution)/shard_map/edges/pallas_call | solution.py:426
  13.2 0.7 collective-permute-start.1
  13.9 35.2 %collective-permute-start.2 = (bf16[3,64,128]{2,1,0:T(8,128)(2,1)S(1)}, bf16[3,64,128]{2,1,0:T(8,128)(2,1)S(1)}, u32[]{:S(2)}, u32[]{:S(2)}) collective-permute-start(bf16[3,64,128]{2,1,0:T(8,128)(2,1)S(1)} %get-tuple-element.26), channel_id=1, source_target_pairs={{8,16},{16,8},{24,32},{32,24},{40,48},{48,40},{56,64},{64,56},{72,... | collective-permute-start | bytes 147464 | tf_op jit(solution)/shard_map/ppermute | solution.py:443
  49.1 0.0 copy-done
  49.1 0.1 inner.1
  49.2 0.0 collective-permute-done.1.rest_ref
  49.2 1.3 %collective-permute-done.2.far_ref = bf16[3,64,128]{2,1,0:T(8,128)(2,1)S(1)} collective-permute-done((bf16[3,64,128]{2,1,0:T(8,128)(2,1)S(1)}, bf16[3,64,128]{2,1,0:T(8,128)(2,1)S(1)}, u32[]{:S(2)}, u32[]{:S(2)}) %collective-permute-start.2) | collective-permute-done | bytes 49184 | tf_op jit(solution)/shard_map/ppermute | solution.py:443
  50.6 0.0 copy-start.2
  50.6 1.8 %outer.1 = (bf16[8,256,128]{2,1,0:T(8,128)(2,1)S(1)}, bf16[8,64,128]{2,1,0:T(8,128)(2,1)}) custom-call(s32[1]{0:T(128)} %bitcast.1.side_ref, s32[1]{0:T(128)} %bitcast.2.lead_ref, bf16[3,64,128]{2,1,0:T(8,128)(2,1)S(1)} %collective-permute-done.first_ref.near_ref, bf16[3,64,128]{2,1,0:T(8,128)(2,1)S(1)} %collective-permute-done.1.rest_ref, ...), custom_call_target="tpu_custom_call" | custom-call | tf_op jit(solution)/shard_map/outer/pallas_call | solution.py:458
  52.3 8.5 %collective-permute-start.3 = (bf16[8,256,128]{2,1,0:T(8,128)(2,1)S(1)}, bf16[8,256,128]{2,1,0:T(8,128)(2,1)S(1)}, u32[]{:S(2)}, u32[]{:S(2)}) collective-permute-start(bf16[8,256,128]{2,1,0:T(8,128)(2,1)S(1)} %get-tuple-element.34.hidden_ref), channel_id=1, source_target_pairs={{0,1},{1,0},{2,3},{3,2},{4,5},{5,4},{6,7},{7,6},{8,9},{9,8},{10,11... | collective-permute-start | bytes 1572872 | tf_op jit(solution)/shard_map/ppermute | solution.py:469
  60.9 2.0 %collective-permute-start.4 = (bf16[8,192,128]{2,1,0:T(8,128)(2,1)S(1)}, bf16[8,192,128]{2,1,0:T(8,128)(2,1)S(1)}, u32[]{:S(2)}, u32[]{:S(2)}) collective-permute-start(bf16[8,192,128]{2,1,0:T(8,128)(2,1)S(1)} %get-tuple-element.28.mid_in), channel_id=1, source_target_pairs={{1,2},{2,1},{3,4},{4,3},{5,6},{6,5},{257,258},{258,257},{259,260},... | collective-permute-start | bytes 1179656 | tf_op jit(solution)/shard_map/ppermute | solution.py:425
  62.8 0.7 collective-permute-start.5
  63.5 3.7 %collective-permute-start.6 = (bf16[8,64,128]{2,1,0:T(8,128)(2,1)}, bf16[8,64,128]{2,1,0:T(8,128)(2,1)}, u32[]{:S(2)}, u32[]{:S(2)}) collective-permute-start(bf16[8,64,128]{2,1,0:T(8,128)(2,1)} %get-tuple-element.35), channel_id=1, source_target_pairs={{1,2},{2,1},{3,4},{4,3},{5,6},{6,5},{9,10},{10,9},{11,12},{12,11},... | collective-permute-start | bytes 393224 | tf_op jit(solution)/shard_map/ppermute | solution.py:468
  67.2 4.3 %collective-permute-done.6.edge_ref = bf16[8,64,128]{2,1,0:T(8,128)(2,1)} collective-permute-done((bf16[8,64,128]{2,1,0:T(8,128)(2,1)}, bf16[8,64,128]{2,1,0:T(8,128)(2,1)}, u32[]{:S(2)}, u32[]{:S(2)}) %collective-permute-start.6) | collective-permute-done | bytes 131104 | tf_op jit(solution)/shard_map/ppermute | solution.py:468
  71.5 0.0 collective-permute-done.4.lead_ref
  71.5 0.0 collective-permute-done.5.rest_ref
  71.5 0.0 copy-done.2
  71.5 1.5 %partial.1.partial_ref = f32[4,256,256]{2,1,0:T(8,128)S(1)} custom-call(s32[1]{0:T(128)} %bitcast.side_ref, bf16[8,256,128]{2,1,0:T(8,128)(2,1)S(1)} %get-tuple-element.34.hidden_ref, bf16[8,192,128]{2,1,0:T(8,128)(2,1)S(1)} %collective-permute-done.4.lead_ref, bf16[8,192,128]{2,1,0:T(8,128)(2,1)S(1)} %collective-permute-done.5.rest_ref, ...), custom_call_target="tpu_custom_call" | custom-call | tf_op jit(solution)/shard_map/partial/pallas_call | solution.py:470
  73.1 0.0 collective-permute-done.3.near_ref
  73.1 1.3 %final.1 = bf16[8,8,32,128]{3,2,1,0:T(8,128)(2,1)} custom-call(s32[1]{0:T(128)} %bitcast.side_ref, bf16[8,256,128]{2,1,0:T(8,128)(2,1)S(1)} %collective-permute-done.3.near_ref, f32[4,256,256]{2,1,0:T(8,128)S(1)} %partial.1.partial_ref, bf16[3,3,128,128]{3,2,1,0:T(8,128)(2,1)S(1)} %copy-done.2, bf16[8,8,32,128]{3,2,1,0:T(8,128)(2,1)S(1)} %copy-done.1), custom_call_target="tpu_custom_call" | custom-call | tf_op jit(solution)/shard_map/final/pallas_call | solution.py:478
Async XLA Ops:
  0.0 10.8 %copy-start.1 = (bf16[8,8,32,128]{3,2,1,0:T(8,128)(2,1)S(1)}, bf16[8,8,32,128]{3,2,1,0:T(8,128)(2,1)}, u32[]{:S(2)}) copy-start(bf16[8,8,32,128]{3,2,1,0:T(8,128)(2,1)} %field_ref.5) | copy-start | bytes 1572868
  5.9 4.9 %collective-permute-start = (bf16[3,64,128]{2,1,0:T(8,128)(2,1)S(1)}, bf16[3,64,128]{2,1,0:T(8,128)(2,1)S(1)}, u32[]{:S(2)}, u32[]{:S(2)}) collective-permute-start(bf16[3,64,128]{2,1,0:T(8,128)(2,1)S(1)} %get-tuple-element.21), channel_id=1, source_target_pairs={{0,8},{8,0},{1,9},{9,1},{2,10},{10,2},{3,11},{11,3},{4,12},{12,4},... | collective-permute-start | bytes 147464 | tf_op jit(solution)/shard_map/ppermute | solution.py:424
  10.8 38.3 %copy-start = (bf16[3,3,3,128,128]{4,3,2,1,0:T(8,128)(2,1)S(1)}, bf16[3,3,3,128,128]{4,3,2,1,0:T(8,128)(2,1)}, u32[]{:S(2)}) copy-start(bf16[3,3,3,128,128]{4,3,2,1,0:T(8,128)(2,1)} %weight_ref.5) | copy-start | bytes 2654212
  13.2 36.0 %collective-permute-start.1 = (bf16[3,64,128]{2,1,0:T(8,128)(2,1)S(1)}, bf16[3,64,128]{2,1,0:T(8,128)(2,1)S(1)}, u32[]{:S(2)}, u32[]{:S(2)}) collective-permute-start(bf16[3,64,128]{2,1,0:T(8,128)(2,1)S(1)} %get-tuple-element.25), channel_id=1, source_target_pairs={{16,24},{24,16},{32,40},{40,32},{48,56},{56,48},{64,72},{72,64},{8... | collective-permute-start | bytes 147464 | tf_op jit(solution)/shard_map/ppermute | solution.py:444
  13.9 36.7 %collective-permute-start.2 = (bf16[3,64,128]{2,1,0:T(8,128)(2,1)S(1)}, bf16[3,64,128]{2,1,0:T(8,128)(2,1)S(1)}, u32[]{:S(2)}, u32[]{:S(2)}) collective-permute-start(bf16[3,64,128]{2,1,0:T(8,128)(2,1)S(1)} %get-tuple-element.26), channel_id=1, source_target_pairs={{8,16},{16,8},{24,32},{32,24},{40,48},{48,40},{56,64},{64,56},{72,... | collective-permute-start | bytes 147464 | tf_op jit(solution)/shard_map/ppermute | solution.py:443
  50.6 21.0 %copy-start.2 = (bf16[3,3,128,128]{3,2,1,0:T(8,128)(2,1)S(1)}, bf16[3,3,128,128]{3,2,1,0:T(8,128)(2,1)}, u32[]{:S(2)}) copy-start(bf16[3,3,128,128]{3,2,1,0:T(8,128)(2,1)} %weight_ref.7) | copy-start | bytes 884740
  52.3 20.8 %collective-permute-start.3 = (bf16[8,256,128]{2,1,0:T(8,128)(2,1)S(1)}, bf16[8,256,128]{2,1,0:T(8,128)(2,1)S(1)}, u32[]{:S(2)}, u32[]{:S(2)}) collective-permute-start(bf16[8,256,128]{2,1,0:T(8,128)(2,1)S(1)} %get-tuple-element.34.hidden_ref), channel_id=1, source_target_pairs={{0,1},{1,0},{2,3},{3,2},{4,5},{5,4},{6,7},{7,6},{8,9},{9,8},{10,11... | collective-permute-start | bytes 1572872 | tf_op jit(solution)/shard_map/ppermute | solution.py:469
  60.9 10.6 %collective-permute-start.4 = (bf16[8,192,128]{2,1,0:T(8,128)(2,1)S(1)}, bf16[8,192,128]{2,1,0:T(8,128)(2,1)S(1)}, u32[]{:S(2)}, u32[]{:S(2)}) collective-permute-start(bf16[8,192,128]{2,1,0:T(8,128)(2,1)S(1)} %get-tuple-element.28.mid_in), channel_id=1, source_target_pairs={{1,2},{2,1},{3,4},{4,3},{5,6},{6,5},{257,258},{258,257},{259,260},... | collective-permute-start | bytes 1179656 | tf_op jit(solution)/shard_map/ppermute | solution.py:425
  62.8 8.7 %collective-permute-start.5 = (bf16[8,192,128]{2,1,0:T(8,128)(2,1)S(1)}, bf16[8,192,128]{2,1,0:T(8,128)(2,1)S(1)}, u32[]{:S(2)}, u32[]{:S(2)}) collective-permute-start(bf16[8,192,128]{2,1,0:T(8,128)(2,1)S(1)} %get-tuple-element.31.mid_ref), channel_id=1, source_target_pairs={{9,10},{10,9},{11,12},{12,11},{13,14},{14,13},{17,18},{18,17},{19,... | collective-permute-start | bytes 1179656 | tf_op jit(solution)/shard_map/ppermute | solution.py:457
  63.5 8.0 %collective-permute-start.6 = (bf16[8,64,128]{2,1,0:T(8,128)(2,1)}, bf16[8,64,128]{2,1,0:T(8,128)(2,1)}, u32[]{:S(2)}, u32[]{:S(2)}) collective-permute-start(bf16[8,64,128]{2,1,0:T(8,128)(2,1)} %get-tuple-element.35), channel_id=1, source_target_pairs={{1,2},{2,1},{3,4},{4,3},{5,6},{6,5},{9,10},{10,9},{11,12},{12,11},... | collective-permute-start | bytes 393224 | tf_op jit(solution)/shard_map/ppermute | solution.py:468
